TPU v7x, 256 devices: a whole 4x4x8 slice. The times are simulated.
256 devices in a mesh: lon: 16 (over y_hi, z), day: 16 (over x, y_lo, core).
Axes of the slice: x: 4, y: 4 (y_hi: 2, y_lo: 2; y = y_hi * 2 + y_lo), z: 8, core: 2. Of those that a mesh axis runs over, the one named last changes fastest.
Arguments:
- field: bfloat16 [368, 1440, 1024], P('day', 'lon'), may hold values from -6 to 6
Outputs:
- filtered: float32 [368, 1440, 1024], P('day', 'lon')
All inputs are finite; a program needn't handle non-finite values.
Results may differ from a plain program's by a relative error of at most 0.0003.
Values may be sent and summed in bfloat16 or wider, within the bound.
No kernel may reach another device: no remote copies, remote signals or barrier semaphores. Data moves between devices by JAX's collectives and lax.ppermute only.
A program may use at most 192 MiB of HBM per device.

v0:
```python
import jax
import jax.numpy as jnp
from jax import lax
from jax.sharding import PartitionSpec as P

DAY_HALF = 15
LON_HALF = 10


def extended(cells, sides, width):
    for axis, dim in sides:
        count = lax.axis_size(axis)
        head = lax.slice_in_dim(cells, 0, width, axis=dim)
        tail = lax.slice_in_dim(cells, cells.shape[dim] - width, cells.shape[dim], axis=dim)
        cells = jnp.concatenate(
            [
                lax.ppermute(tail, axis, [(i, (i + 1) % count) for i in range(count)]),
                cells,
                lax.ppermute(head, axis, [((i + 1) % count, i) for i in range(count)]),
            ],
            axis=dim,
        )
    return cells


def running(values, dim, half):
    count = values.shape[dim] - 2 * half
    total = jnp.cumsum(values, axis=dim)
    first = jnp.zeros_like(lax.slice_in_dim(total, 0, 1, axis=dim))
    total = jnp.concatenate([first, total], axis=dim)
    upper = lax.slice_in_dim(total, 2 * half + 1, 2 * half + 1 + count, axis=dim)
    lower = lax.slice_in_dim(total, 0, count, axis=dim)
    return (upper - lower) / (2.0 * half + 1.0)


def local(field):
    tall = extended(field, (("day", 0),), DAY_HALF)
    values = tall.astype(jnp.float32)
    clim = running(values, 0, DAY_HALF)
    anomaly = values[DAY_HALF : values.shape[0] - DAY_HALF] - clim
    padded = extended(anomaly, (("lon", 1),), LON_HALF)
    return running(padded, 1, LON_HALF)


def solution(mesh):
    return jax.shard_map(
        local,
        mesh=mesh,
        in_specs=(P("day", "lon", None),),
        out_specs=P("day", "lon", None),
        check_vma=False,
    )
```

profile of v0, /device:TPU:1, one launch (start us, length us, event | category | flops | bytes accessed | tf_op | source)
XLA Modules:
  0.0 157.4 jit_solution(8249850145674973770)
XLA Ops:
  0.0 4.7 %copy.6 = bf16[23,90,1024]{2,1,0:T(8,128)(2,1)S(1)} copy(bf16[23,90,1024]{2,0,1:T(8,128)(2,1)} %param.1) | data formatting | bytes 8478720 | tf_op args[0]
  4.7 0.0 copy-start.1
  4.7 0.7 fusion.9
  5.5 2.8 %collective-permute-start = (bf16[15,90,1024]{2,1,0:T(8,128)(2,1)S(1)}, bf16[15,90,1024]{2,1,0:T(8,128)(2,1)S(1)}, u32[]{:S(2)}, u32[]{:S(2)}) collective-permute-start(bf16[15,90,1024]{2,1,0:T(8,128)(2,1)S(1)} %get-tuple-element.7), channel_id=1, source_target_pairs={{0,1},{1,2},{2,3},{3,4},{4,5},{5,6},{6,7},{7,8},{8,9},{9,10},{10,1... | collective-permute-start | bytes 8294408 | tf_op jit(solution)/shard_map/ppermute | solution.py:17
  8.2 0.6 collective-permute-start.1
  8.8 63.1 %collective-permute-done = bf16[15,90,1024]{2,1,0:T(8,128)(2,1)S(1)} collective-permute-done((bf16[15,90,1024]{2,1,0:T(8,128)(2,1)S(1)}, bf16[15,90,1024]{2,1,0:T(8,128)(2,1)S(1)}, u32[]{:S(2)}, u32[]{:S(2)}) %collective-permute-start) | collective-permute-done | bytes 2764832 | tf_op jit(solution)/shard_map/ppermute | solution.py:17
  71.9 0.0 copy-start.3
  71.9 2.6 %collective-permute-done.1 = bf16[15,90,1024]{2,1,0:T(8,128)(2,1)} collective-permute-done((bf16[15,90,1024]{2,1,0:T(8,128)(2,1)S(1)}, bf16[15,90,1024]{2,1,0:T(8,128)(2,1)}, u32[]{:S(2)}, u32[]{:S(2)}) %collective-permute-start.1) | collective-permute-done | bytes 2764832 | tf_op jit(solution)/shard_map/ppermute | solution.py:19
  74.5 0.0 copy-done.1
  74.5 0.0 copy-done.3
  74.5 8.7 %fusion.7 = f32[53,90,1024]{2,1,0:T(8,128)} fusion(bf16[15,90,1024]{2,1,0:T(8,128)(2,1)} %collective-permute-done.1, bf16[23,90,1024]{2,1,0:T(8,128)(2,1)S(1)} %copy.6, bf16[15,90,1024]{2,1,0:T(8,128)(2,1)S(1)} %collective-permute-done), kind=kOutput, calls=%fused_computation.11 | output fusion | flops 268646400 | bytes 29306880 | tf_op jit(solution)/shard_map/jit(cumsum)/reduce_window_sum | solution.py:28
  83.2 0.0 copy-start
  83.2 13.1 %maximum_convert_fusion = f32[53,90,1024]{2,1,0:T(8,128)} fusion(bf16[15,90,1024]{2,1,0:T(8,128)(2,1)} %collective-permute-done.1, bf16[23,90,1024]{2,1,0:T(8,128)(2,1)} %copy-done.1, bf16[15,90,1024]{2,1,0:T(8,128)(2,1)} %copy-done.3), kind=kLoop, calls=%fused_computation.5 | loop fusion | flops 14653440 | bytes 29306880 | tf_op jit(solution)/shard_map/convert_element_type | solution.py:38
  96.3 4.5 %copy-done = f32[53,90,1024]{2,1,0:T(8,128)S(1)} copy-done((f32[53,90,1024]{2,1,0:T(8,128)S(1)}, f32[53,90,1024]{2,1,0:T(8,128)}, u32[]{:S(2)}) %copy-start) | copy-done | bytes 19537944
  100.8 7.7 %fusion.4 = f32[23,90,1024]{2,1,0:T(8,128)} fusion(f32[53,90,1024]{2,1,0:T(8,128)S(1)} %copy-done, f32[53,90,1024]{2,1,0:T(8,128)} %maximum_convert_fusion), kind=kLoop, calls=%fused_computation.8 | loop fusion | flops 6359040 | bytes 46841856 | tf_op jit(solution)/shard_map/sub | solution.py:40
  108.5 0.0 copy-start.2
  108.5 2.2 %fusion.8 = (f32[23,10,1024]{2,1,0:T(8,128)S(1)}, f32[23,10,1024]{2,1,0:T(8,128)S(1)}) fusion(f32[23,90,1024]{2,1,0:T(8,128)} %fusion.4), kind=kLoop, calls=%fused_computation.12 | loop fusion | bytes 3768320 | tf_op jit(solution)/shard_map/slice | solution.py:14
  110.7 0.6 copy.10
  111.3 8.0 %collective-permute-start.3 = (f32[23,10,1024]{2,0,1:T(8,128)S(1)}, f32[23,10,1024]{2,0,1:T(8,128)S(1)}, u32[]{:S(2)}, u32[]{:S(2)}) collective-permute-start(f32[23,10,1024]{2,0,1:T(8,128)S(1)} %copy.10), channel_id=1, source_target_pairs={{16,0},{32,16},{48,32},{64,48},{80,64},{96,80},{112,96},{128,112},... | collective-permute-start | bytes 2826248 | tf_op jit(solution)/shard_map/ppermute | solution.py:19
  119.3 0.6 copy.9
  119.8 0.3 collective-permute-start.2
  120.1 10.2 %collective-permute-done.3 = f32[23,10,1024]{2,0,1:T(8,128)S(1)} collective-permute-done((f32[23,10,1024]{2,0,1:T(8,128)S(1)}, f32[23,10,1024]{2,0,1:T(8,128)S(1)}, u32[]{:S(2)}, u32[]{:S(2)}) %collective-permute-start.3) | collective-permute-done | bytes 942112 | tf_op jit(solution)/shard_map/ppermute | solution.py:19
  130.3 0.6 copy.12
  130.9 5.7 %collective-permute-done.2 = f32[23,10,1024]{2,0,1:T(8,128)S(1)} collective-permute-done((f32[23,10,1024]{2,0,1:T(8,128)S(1)}, f32[23,10,1024]{2,0,1:T(8,128)S(1)}, u32[]{:S(2)}, u32[]{:S(2)}) %collective-permute-start.2) | collective-permute-done | bytes 942112 | tf_op jit(solution)/shard_map/ppermute | solution.py:17
  136.7 0.6 copy.11
  137.2 0.0 copy-done.2
  137.2 4.8 %pad_maximum_fusion = f32[23,110,1024]{2,1,0:T(8,128)} fusion(f32[23,10,1024]{2,1,0:T(8,128)S(1)} %copy.12, f32[23,90,1024]{2,1,0:T(8,128)S(1)} %copy-done.2, f32[23,10,1024]{2,1,0:T(8,128)S(1)} %copy.11), kind=kLoop, calls=%fused_computation.4 | loop fusion | flops 5181440 | bytes 20725760 | tf_op jit(solution)/shard_map/concatenate | solution.py:15
  142.1 10.7 %fusion = f32[23,110,1024]{2,0,1:T(8,128)S(1)} fusion(f32[23,110,1024]{2,1,0:T(8,128)} %pad_maximum_fusion), kind=kOutput, calls=%fused_computation.2 | output fusion | flops 282388480 | bytes 20725760 | tf_op jit(solution)/shard_map/jit(cumsum)/reduce_window_sum | solution.py:28
  152.7 4.6 %fusion.6 = f32[23,90,1024]{2,0,1:T(8,128)} fusion(f32[23,110,1024]{2,0,1:T(8,128)S(1)} %fusion), kind=kLoop, calls=%fused_computation.10 | loop fusion | flops 4239360 | bytes 28139520 | tf_op jit(solution)/shard_map/div | solution.py:33
Async XLA Ops:
  4.7 69.8 %copy-start.1 = (bf16[23,90,1024]{2,1,0:T(8,128)(2,1)}, bf16[23,90,1024]{2,1,0:T(8,128)(2,1)S(1)}, u32[]{:S(2)}) copy-start(bf16[23,90,1024]{2,1,0:T(8,128)(2,1)S(1)} %copy.6) | copy-start | bytes 12718084
  5.5 66.5 %collective-permute-start = (bf16[15,90,1024]{2,1,0:T(8,128)(2,1)S(1)}, bf16[15,90,1024]{2,1,0:T(8,128)(2,1)S(1)}, u32[]{:S(2)}, u32[]{:S(2)}) collective-permute-start(bf16[15,90,1024]{2,1,0:T(8,128)(2,1)S(1)} %get-tuple-element.7), channel_id=1, source_target_pairs={{0,1},{1,2},{2,3},{3,4},{4,5},{5,6},{6,7},{7,8},{8,9},{9,10},{10,1... | collective-permute-start | bytes 8294408 | tf_op jit(solution)/shard_map/ppermute | solution.py:17
  8.2 66.3 %collective-permute-start.1 = (bf16[15,90,1024]{2,1,0:T(8,128)(2,1)S(1)}, bf16[15,90,1024]{2,1,0:T(8,128)(2,1)}, u32[]{:S(2)}, u32[]{:S(2)}) collective-permute-start(bf16[15,90,1024]{2,1,0:T(8,128)(2,1)S(1)} %get-tuple-element.8), channel_id=1, source_target_pairs={{1,0},{2,1},{3,2},{4,3},{5,4},{6,5},{7,6},{8,7},{9,8},{10,9},{11,1... | collective-permute-start | bytes 8294408 | tf_op jit(solution)/shard_map/ppermute | solution.py:19
  71.9 2.6 %copy-start.3 = (bf16[15,90,1024]{2,1,0:T(8,128)(2,1)}, bf16[15,90,1024]{2,1,0:T(8,128)(2,1)S(1)}, u32[]{:S(2)}) copy-start(bf16[15,90,1024]{2,1,0:T(8,128)(2,1)S(1)} %collective-permute-done) | copy-start | bytes 8294404
  83.2 17.6 %copy-start = (f32[53,90,1024]{2,1,0:T(8,128)S(1)}, f32[53,90,1024]{2,1,0:T(8,128)}, u32[]{:S(2)}) copy-start(f32[53,90,1024]{2,1,0:T(8,128)} %fusion.7) | copy-start | bytes 58613764
  108.5 28.7 %copy-start.2 = (f32[23,90,1024]{2,1,0:T(8,128)S(1)}, f32[23,90,1024]{2,1,0:T(8,128)}, u32[]{:S(2)}) copy-start(f32[23,90,1024]{2,1,0:T(8,128)} %fusion.4) | copy-start | bytes 25436164
  111.3 19.0 %collective-permute-start.3 = (f32[23,10,1024]{2,0,1:T(8,128)S(1)}, f32[23,10,1024]{2,0,1:T(8,128)S(1)}, u32[]{:S(2)}, u32[]{:S(2)}) collective-permute-start(f32[23,10,1024]{2,0,1:T(8,128)S(1)} %copy.10), channel_id=1, source_target_pairs={{16,0},{32,16},{48,32},{64,48},{80,64},{96,80},{112,96},{128,112},... | collective-permute-start | bytes 2826248 | tf_op jit(solution)/shard_map/ppermute | solution.py:19
  119.8 16.8 %collective-permute-start.2 = (f32[23,10,1024]{2,0,1:T(8,128)S(1)}, f32[23,10,1024]{2,0,1:T(8,128)S(1)}, u32[]{:S(2)}, u32[]{:S(2)}) collective-permute-start(f32[23,10,1024]{2,0,1:T(8,128)S(1)} %copy.9), channel_id=1, source_target_pairs={{0,16},{16,32},{32,48},{48,64},{64,80},{80,96},{96,112},{112,128},... | collective-permute-start | bytes 2826248 | tf_op jit(solution)/shard_map/ppermute | solution.py:17
where the time goes:
time: 158 us; the launch traced here: 157 us
  waiting for transfers between devices  81.6 us (52%)
  other arithmetic  49.6 us (31%)
  local copies, waits for them, and re-layouts  14.4 us (9%)
  starting transfers between devices  11.6 us (7%)
    ppermute x2, waiting for transfers between devices, extended(): lax.ppermute(tail, axis, [(i, (i + 1) % count) for i in range(count)])  68.8 us
    another operation x2, other arithmetic, running(): total = jnp.cumsum(values, axis=dim)  19.4 us
    convert_element_type x1, other arithmetic, local(): values = tall.astype(jnp.float32)  13.1 us
    ppermute x2, waiting for transfers between devices, extended(): lax.ppermute(head, axis, [((i + 1) % count, i) for i in range(count)])  12.8 us
    unnamed x9, local copies, waits for them, and re-layouts  9.21 us
    ppermute x2, starting transfers between devices, extended(): lax.ppermute(head, axis, [((i + 1) % count, i) for i in range(count)])  8.6 us
    sub x1, other arithmetic, local(): anomaly = values[DAY_HALF:values.shape[0] - DAY_HALF] - clim  7.71 us
    concatenate x1, other arithmetic, extended(): jnp.concatenate([lax.ppermute(tail, axis, [(i, (i + 1) % count) for i in...  4.81 us
  transfers between devices with their start and end apart: 4, of which 4 were waited for; matrix products, arithmetic and copies ran while one was open for 1% of the time, Pallas kernels for 0%

commit v1 on v0

v1 whole, which is shorter than its diff:
```python
import functools

import jax
import jax.numpy as jnp
from jax import lax
from jax.experimental import pallas as pl
from jax.experimental.pallas import tpu as pltpu
from jax.sharding import PartitionSpec as P

DAY_HALF = 15
LON_HALF = 10
DAY_PAD = 16
DAY_WIN = 2 * DAY_HALF + 1
LON_WIN = 2 * LON_HALF + 1
SCALE = 1.0 / (DAY_WIN * LON_WIN)
BLOCK = 256
WIDTHS = (256, 256, 256, 256)
VMEM = pl.BlockSpec(memory_space=pltpu.VMEM)


def day_matrices(days):
    def part(count, first):
        d = lax.broadcasted_iota(jnp.int32, (days, count), 0)
        s = lax.broadcasted_iota(jnp.int32, (days, count), 1) + first
        near = (s - d <= DAY_HALF) & (d - s <= DAY_HALF)
        return (jnp.where(s == d, float(DAY_WIN), 0.0) - jnp.where(near, 1.0, 0.0)).astype(jnp.bfloat16)

    return part(DAY_HALF, -DAY_HALF), part(days, 0), part(DAY_HALF, days)


def dot(a, b):
    return jnp.dot(a, b, preferred_element_type=jnp.float32)


def pack_kernel(groups, start, own, fwd, bwd):
    days, width = own.shape[1], fwd.shape[2]
    cols = slice(start, start + width)
    to = 0
    for first, count in groups:
        at, to = slice(to, to + count), to + count
        src = slice(first, first + count)
        fwd[at, :DAY_HALF, :] = own[src, days - DAY_HALF : days, cols]
        bwd[at, :DAY_HALF, :] = own[src, :DAY_HALF, cols]


def edge_kernel(field, left, right, to_right, to_left):
    lons, days, width = field.shape
    high = lons - LON_HALF
    ml, mo, mr = day_matrices(days)
    for c in range(width // BLOCK):
        cols = slice(c * BLOCK, (c + 1) * BLOCK)

        def anomaly(i):
            own = field[i if i < LON_HALF else high + i - LON_HALF, :, cols]
            halo_l = left[i, :DAY_HALF, cols]
            halo_r = right[i, :DAY_HALF, cols]
            return dot(ml, halo_l) + dot(mo, own) + dot(mr, halo_r)

        total = anomaly(0)
        to_left[0, :, cols] = total
        for j in range(1, LON_HALF):
            total = total + anomaly(j)
            to_left[j, :, cols] = total
        total = anomaly(2 * LON_HALF - 1)
        to_right[LON_HALF - 1, :, cols] = total
        for j in range(LON_HALF - 2, -1, -1):
            total = total + anomaly(LON_HALF + j)
            to_right[j, :, cols] = total


def main_kernel(start, own, edge_l, edge_r, mid_l, mid_r, from_l, from_r, prev, out, g):
    lons, days, _ = own.shape
    width = out.shape[2]
    high = lons - LON_HALF
    cols = slice(start, start + width)
    ml, mo, mr = day_matrices(days)

    def anomaly(l, left, right):
        g[l] = dot(ml, left) + dot(mo, own[l, :, cols]) + dot(mr, right)

    for l in range(LON_HALF):
        for at, e in ((l, l), (high + l, LON_HALF + l)):
            anomaly(at, edge_l[e, :DAY_HALF, cols], edge_r[e, :DAY_HALF, cols])

    def inner(i, _):
        anomaly(LON_HALF + i, mid_l[i, :DAY_HALF, :], mid_r[i, :DAY_HALF, :])
        return 0

    lax.fori_loop(0, high - LON_HALF, inner, 0, unroll=10)

    total = g[0]
    for l in range(1, LON_HALF):
        total = total + g[l]

    def first(l, total):
        total = total + g[l + LON_HALF]
        out[l] = (total + from_l[l, :, cols]) * SCALE
        return total

    def center(l, total):
        total = total + (g[l + LON_HALF] - g[l - LON_HALF - 1])
        out[l] = total * SCALE
        return total

    def last(l, total):
        total = total - g[l - LON_HALF - 1]
        out[l] = (total + from_r[l - high, :, cols]) * SCALE
        return total

    total = lax.fori_loop(0, LON_HALF, first, total, unroll=True)
    total = total + g[2 * LON_HALF]
    out[LON_HALF] = total * SCALE
    total = lax.fori_loop(LON_HALF + 1, high, center, total, unroll=3)
    lax.fori_loop(high, lons, last, total, unroll=True)


def local(field):
    field = jnp.transpose(field, (1, 0, 2))
    lons, days, cols = field.shape
    high = lons - LON_HALF
    mid = high - LON_HALF
    nday, nlon = lax.axis_size("day"), lax.axis_size("lon")
    params = pltpu.CompilerParams(vmem_limit_bytes=24 * 2**20)
    starts = [sum(WIDTHS[:c]) for c in range(len(WIDTHS))]

    def cost(work):
        return pl.CostEstimate(flops=10**3 * work, bytes_accessed=10 * work, transcendentals=0)

    def shift(x, axis, n, step):
        return lax.ppermute(x, axis, [(i, (i + step) % n) for i in range(n)])

    def halos(packed):
        fwd, bwd = packed
        return shift(fwd, "day", nday, 1), shift(bwd, "day", nday, -1)

    def pack(groups, start, width):
        shape = (sum(n for _, n in groups), DAY_PAD, width)
        packed = pl.pallas_call(
            functools.partial(pack_kernel, groups, start),
            in_specs=[VMEM],
            out_specs=[VMEM] * 2,
            out_shape=[jax.ShapeDtypeStruct(shape, field.dtype)] * 2,
            cost_estimate=cost(1000),
            compiler_params=params,
        )(field)
        return halos(packed)

    edge_l, edge_r = pack(((0, LON_HALF), (high, LON_HALF)), 0, cols)
    mids = [pack(((LON_HALF, mid),), starts[c], w) for c, w in enumerate(WIDTHS)]

    to_right, to_left = pl.pallas_call(
        edge_kernel,
        in_specs=[VMEM] * 3,
        out_specs=[VMEM] * 2,
        out_shape=[jax.ShapeDtypeStruct((LON_HALF, days, cols), jnp.float32)] * 2,
        cost_estimate=cost(5000),
        compiler_params=params,
        name="edge",
    )(field, edge_l, edge_r)
    from_l = shift(to_right, "lon", nlon, 1)
    from_r = shift(to_left, "lon", nlon, -1)

    out = None
    for c, width in enumerate(WIDTHS):
        at = pl.BlockSpec((lons, days, width), lambda i, c=c: (0, 0, starts[c] // WIDTHS[c]))
        specs = [VMEM] * 7
        args = [field, edge_l, edge_r, *mids[c], from_l, from_r]
        body = functools.partial(main_kernel, starts[c])
        if c:
            specs.append(pl.BlockSpec(memory_space=pl.ANY))
            args.append(out)
            fn, alias = body, {7: 0}
        else:
            fn, alias = lambda *refs, body=body: body(*refs[:7], None, *refs[7:]), {}
        out = pl.pallas_call(
            fn,
            grid=(1,),
            in_specs=specs,
            out_specs=at,
            out_shape=jax.ShapeDtypeStruct(field.shape, jnp.float32),
            input_output_aliases=alias,
            scratch_shapes=[pltpu.VMEM((lons, days, width), jnp.float32)],
            cost_estimate=cost(5000),
            compiler_params=params,
        )(*args)
    return jnp.transpose(out, (1, 0, 2))


def solution(mesh):
    return jax.shard_map(
        local,
        mesh=mesh,
        in_specs=(P("day", "lon", None),),
        out_specs=P("day", "lon", None),
        check_vma=False,
    )
```

time: 158 us -> 102 us (0.65)
  other arithmetic: 49.6 us -> 0 us
  waiting for transfers between devices: 81.6 us -> 63.2 us
  Pallas kernels: 0 us -> 18.3 us
  local copies, waits for them, and re-layouts: 14.4 us -> 2.25 us
  starting transfers between devices: 11.6 us -> 17.7 us
    another operation x2 -> x0, other arithmetic: 19.4 us -> none  [running(): total = jnp.cumsum(values, axis=dim)]
    ppermute x4 -> x12, waiting for transfers between devices: 81.6 us -> 63.2 us  [shift(): return lax.ppermute(x, axis, [(i, (i + step) % n) for i in range(n)])]
    pallas_call x0 -> x10, Pallas kernels: none -> 18.3 us  [the longest x4 16.5 us: local(): pl.pallas_call(fn, grid=(1,), in_specs=specs, out_specs=at, out_shape=jax...]
    convert_element_type x1 -> x0, other arithmetic: 13.1 us -> none  [local(): values = tall.astype(jnp.float32)]
    sub x1 -> x0, other arithmetic: 7.71 us -> none  [local(): anomaly = values[DAY_HALF:values.shape[0] - DAY_HALF] - clim]
    unnamed x9 -> x2, local copies, waits for them, and re-layouts: 9.21 us -> 2.25 us
    ppermute x4 -> x12, starting transfers between devices: 11.6 us -> 17.7 us  [shift(): return lax.ppermute(x, axis, [(i, (i + step) % n) for i in range(n)])]
    concatenate x1 -> x0, other arithmetic: 4.81 us -> none  [extended(): jnp.concatenate([lax.ppermute(tail, axis, [(i, (i + 1) % count) for i in...]
  transfers between devices with their start and end apart: 4 -> 12, of which waited for: 4 -> 8; matrix products, arithmetic and copies ran while one was open for 1% -> 0% of each run, Pallas kernels for 0% -> 13%
where the time goes in v1:
time: 102 us; the launch traced here: 101 us
  waiting for transfers between devices  63.2 us (62%)
  Pallas kernels  18.3 us (18%)
  starting transfers between devices  17.7 us (17%)
  local copies, waits for them, and re-layouts  2.25 us (2%)
    ppermute x12, waiting for transfers between devices, shift(): return lax.ppermute(x, axis, [(i, (i + step) % n) for i in range(n)])  63.2 us
    ppermute x12, starting transfers between devices, shift(): return lax.ppermute(x, axis, [(i, (i + step) % n) for i in range(n)])  17.7 us
    pallas_call x4, Pallas kernels, local(): pl.pallas_call(fn, grid=(1,), in_specs=specs, out_specs=at, out_shape=jax...  16.5 us
    unnamed x2, local copies, waits for them, and re-layouts  2.25 us
  transfers between devices with their start and end apart: 12, of which 8 were waited for; matrix products, arithmetic and copies ran while one was open for 0% of the time, Pallas kernels for 13%

profile of v1, /device:TPU:1, one launch (start us, length us, event | category | flops | bytes accessed | tf_op | source)
XLA Modules:
  0.0 101.5 jit_solution(3741193475350712141)
XLA Ops:
  0.0 2.3 %copy-done = bf16[23,90,1024]{2,0,1:T(8,128)(2,1)S(1)} copy-done((bf16[23,90,1024]{2,0,1:T(8,128)(2,1)S(1)}, bf16[23,90,1024]{2,0,1:T(8,128)(2,1)}, u32[]{:S(2)}) %copy-start) | copy-done | bytes 4239384
  2.3 0.1 shard_map.17
  2.4 2.8 %collective-permute-start = (bf16[20,16,1024]{2,1,0:T(8,128)(2,1)S(1)}, bf16[20,16,1024]{2,1,0:T(8,128)(2,1)S(1)}, u32[]{:S(2)}, u32[]{:S(2)}) collective-permute-start(bf16[20,16,1024]{2,1,0:T(8,128)(2,1)S(1)} %get-tuple-element.17), channel_id=1, source_target_pairs={{0,1},{1,2},{2,3},{3,4},{4,5},{5,6},{6,7},{7,8},{8,9},{9,10},{10,1... | collective-permute-start | bytes 1966088 | tf_op jit(solution)/shard_map/ppermute | solution.py:130
  5.1 0.6 collective-permute-start.1
  5.7 13.9 %collective-permute-done.left.refs_1_.edge_l = bf16[20,16,1024]{2,1,0:T(8,128)(2,1)S(1)} collective-permute-done((bf16[20,16,1024]{2,1,0:T(8,128)(2,1)S(1)}, bf16[20,16,1024]{2,1,0:T(8,128)(2,1)S(1)}, u32[]{:S(2)}, u32[]{:S(2)}) %collective-permute-start) | collective-permute-done | bytes 655392 | tf_op jit(solution)/shard_map/ppermute | solution.py:130
  19.7 2.5 %collective-permute-done.1.right.refs_2_.edge_r = bf16[20,16,1024]{2,1,0:T(8,128)(2,1)S(1)} collective-permute-done((bf16[20,16,1024]{2,1,0:T(8,128)(2,1)S(1)}, bf16[20,16,1024]{2,1,0:T(8,128)(2,1)S(1)}, u32[]{:S(2)}, u32[]{:S(2)}) %collective-permute-start.1) | collective-permute-done | bytes 655392 | tf_op jit(solution)/shard_map/ppermute | solution.py:130
  22.1 1.2 %edge.1 = (f32[10,23,1024]{2,1,0:T(8,128)S(1)}, f32[10,23,1024]{2,1,0:T(8,128)S(1)}) custom-call(bf16[90,23,1024]{2,1,0:T(8,128)(2,1)S(1)} %bitcast.3, bf16[20,16,1024]{2,1,0:T(8,128)(2,1)S(1)} %collective-permute-done.left.refs_1_.edge_l, bf16[20,16,1024]{2,1,0:T(8,128)(2,1)S(1)} %collective-permute-done.1.right.refs_2_.edge_r), custom_call_target="tpu_custom_call" | custom-call | flops 5000000 | bytes 50000 | tf_op jit(solution)/shard_map/edge/pallas_call | solution.py:151
  23.3 2.0 %collective-permute-start.4 = (f32[10,23,1024]{2,1,0:T(8,128)S(1)}, f32[10,23,1024]{2,1,0:T(8,128)S(1)}, u32[]{:S(2)}, u32[]{:S(2)}) collective-permute-start(f32[10,23,1024]{2,1,0:T(8,128)S(1)} %get-tuple-element.21), channel_id=1, source_target_pairs={{0,16},{16,32},{32,48},{48,64},{64,80},{80,96},{96,112},{112,128},... | collective-permute-start | bytes 2826248 | tf_op jit(solution)/shard_map/ppermute | solution.py:130
  25.3 6.4 %collective-permute-start.5 = (f32[10,23,1024]{2,1,0:T(8,128)S(1)}, f32[10,23,1024]{2,1,0:T(8,128)S(1)}, u32[]{:S(2)}, u32[]{:S(2)}) collective-permute-start(f32[10,23,1024]{2,1,0:T(8,128)S(1)} %get-tuple-element.22), channel_id=1, source_target_pairs={{0,240},{16,0},{32,16},{48,32},{64,48},{80,64},{96,80},{112,96},{1... | collective-permute-start | bytes 2826248 | tf_op jit(solution)/shard_map/ppermute | solution.py:130
  31.7 0.1 shard_map.21
  31.8 0.1 collective-permute-start.10
  31.9 0.5 collective-permute-start.11
  32.4 0.2 shard_map.20
  32.6 1.4 %collective-permute-start.8 = (bf16[70,16,256]{2,1,0:T(8,128)(2,1)S(1)}, bf16[70,16,256]{2,1,0:T(8,128)(2,1)S(1)}, u32[]{:S(2)}, u32[]{:S(2)}) collective-permute-start(bf16[70,16,256]{2,1,0:T(8,128)(2,1)S(1)} %get-tuple-element.25), channel_id=1, source_target_pairs={{0,1},{1,2},{2,3},{3,4},{4,5},{5,6},{6,7},{7,8},{8,9},{9,10},{10,1... | collective-permute-start | bytes 1720328 | tf_op jit(solution)/shard_map/ppermute | solution.py:130
  34.0 28.9 %collective-permute-done.10.refs_3_ = bf16[70,16,256]{2,1,0:T(8,128)(2,1)S(1)} collective-permute-done((bf16[70,16,256]{2,1,0:T(8,128)(2,1)S(1)}, bf16[70,16,256]{2,1,0:T(8,128)(2,1)S(1)}, u32[]{:S(2)}, u32[]{:S(2)}) %collective-permute-start.10) | collective-permute-done | bytes 573472 | tf_op jit(solution)/shard_map/ppermute | solution.py:130
  62.9 0.1 shard_map.19
  63.0 1.2 %collective-permute-done.11.refs_4_ = bf16[70,16,256]{2,1,0:T(8,128)(2,1)S(1)} collective-permute-done((bf16[70,16,256]{2,1,0:T(8,128)(2,1)S(1)}, bf16[70,16,256]{2,1,0:T(8,128)(2,1)S(1)}, u32[]{:S(2)}, u32[]{:S(2)}) %collective-permute-start.11) | collective-permute-done | bytes 573472 | tf_op jit(solution)/shard_map/ppermute | solution.py:130
  64.2 1.4 %collective-permute-start.6 = (bf16[70,16,256]{2,1,0:T(8,128)(2,1)S(1)}, bf16[70,16,256]{2,1,0:T(8,128)(2,1)S(1)}, u32[]{:S(2)}, u32[]{:S(2)}) collective-permute-start(bf16[70,16,256]{2,1,0:T(8,128)(2,1)S(1)} %get-tuple-element.23), channel_id=1, source_target_pairs={{0,1},{1,2},{2,3},{3,4},{4,5},{5,6},{6,7},{7,8},{8,9},{9,10},{10,1... | collective-permute-start | bytes 1720328 | tf_op jit(solution)/shard_map/ppermute | solution.py:130
  65.6 9.6 %collective-permute-done.8.mid_l = bf16[70,16,256]{2,1,0:T(8,128)(2,1)S(1)} collective-permute-done((bf16[70,16,256]{2,1,0:T(8,128)(2,1)S(1)}, bf16[70,16,256]{2,1,0:T(8,128)(2,1)S(1)}, u32[]{:S(2)}, u32[]{:S(2)}) %collective-permute-start.8) | collective-permute-done | bytes 573472 | tf_op jit(solution)/shard_map/ppermute | solution.py:130
  75.2 0.0 collective-permute-start.7
  75.2 0.2 shard_map.18
  75.4 2.6 %collective-permute-start.2 = (bf16[70,16,256]{2,1,0:T(8,128)(2,1)S(1)}, bf16[70,16,256]{2,1,0:T(8,128)(2,1)S(1)}, u32[]{:S(2)}, u32[]{:S(2)}) collective-permute-start(bf16[70,16,256]{2,1,0:T(8,128)(2,1)S(1)} %get-tuple-element.19), channel_id=1, source_target_pairs={{0,1},{1,2},{2,3},{3,4},{4,5},{5,6},{6,7},{7,8},{8,9},{9,10},{10,1... | collective-permute-start | bytes 1720328 | tf_op jit(solution)/shard_map/ppermute | solution.py:130
  77.9 0.0 collective-permute-done.5.refs_6_.from_r
  77.9 0.0 collective-permute-start.3
  77.9 4.1 %shard_map.22.prev = f32[90,23,1024]{2,1,0:T(8,128)} custom-call(bf16[90,23,1024]{2,1,0:T(8,128)(2,1)S(1)} %bitcast.8, bf16[20,16,1024]{2,1,0:T(8,128)(2,1)S(1)} %collective-permute-done.left.refs_1_.edge_l, bf16[20,16,1024]{2,1,0:T(8,128)(2,1)S(1)} %collective-permute-done.1.right.refs_2_.edge_r, bf16[70,16,256]{2,1,0:T(8,128)(2,1)S(1)} %collective-permute-done.10.refs_3_, ...), custom_call_target="tpu_custom_call" | custom-call | flops 5000000 | bytes 50000 | tf_op jit(solution)/shard_map/pallas_call | solution.py:175
  82.0 3.0 %collective-permute-done.9.mid_r = bf16[70,16,256]{2,1,0:T(8,128)(2,1)S(1)} collective-permute-done((bf16[70,16,256]{2,1,0:T(8,128)(2,1)S(1)}, bf16[70,16,256]{2,1,0:T(8,128)(2,1)S(1)}, u32[]{:S(2)}, u32[]{:S(2)}) %collective-permute-start.9) | collective-permute-done | bytes 573472 | tf_op jit(solution)/shard_map/ppermute | solution.py:130
  85.1 4.1 %shard_map.23.prev = f32[90,23,1024]{2,1,0:T(8,128)} custom-call(bf16[90,23,1024]{2,1,0:T(8,128)(2,1)S(1)} %bitcast.9, bf16[20,16,1024]{2,1,0:T(8,128)(2,1)S(1)} %collective-permute-done.left.refs_1_.edge_l, bf16[20,16,1024]{2,1,0:T(8,128)(2,1)S(1)} %collective-permute-done.1.right.refs_2_.edge_r, ...), custom_call_target="tpu_custom_call", output_to_operand_aliasing={{}: (7, {})} | custom-call | flops 5000000 | bytes 50000 | tf_op jit(solution)/shard_map/pallas_call | solution.py:175
  89.2 0.0 collective-permute-done.6.mid_l
  89.2 2.0 %collective-permute-done.7.mid_r = bf16[70,16,256]{2,1,0:T(8,128)(2,1)S(1)} collective-permute-done((bf16[70,16,256]{2,1,0:T(8,128)(2,1)S(1)}, bf16[70,16,256]{2,1,0:T(8,128)(2,1)S(1)}, u32[]{:S(2)}, u32[]{:S(2)}) %collective-permute-start.7) | collective-permute-done | bytes 573472 | tf_op jit(solution)/shard_map/ppermute | solution.py:130
  91.2 4.1 %shard_map.24.prev = f32[90,23,1024]{2,1,0:T(8,128)} custom-call(bf16[90,23,1024]{2,1,0:T(8,128)(2,1)S(1)} %bitcast.10, bf16[20,16,1024]{2,1,0:T(8,128)(2,1)S(1)} %collective-permute-done.left.refs_1_.edge_l, bf16[20,16,1024]{2,1,0:T(8,128)(2,1)S(1)} %collective-permute-done.1.right.refs_2_.edge_r, ...), custom_call_target="tpu_custom_call", output_to_operand_aliasing={{}: (7, {})} | custom-call | flops 5000000 | bytes 50000 | tf_op jit(solution)/shard_map/pallas_call | solution.py:175
  95.3 2.0 %collective-permute-done.3.mid_r = bf16[70,16,256]{2,1,0:T(8,128)(2,1)S(1)} collective-permute-done((bf16[70,16,256]{2,1,0:T(8,128)(2,1)S(1)}, bf16[70,16,256]{2,1,0:T(8,128)(2,1)S(1)}, u32[]{:S(2)}, u32[]{:S(2)}) %collective-permute-start.3) | collective-permute-done | bytes 573472 | tf_op jit(solution)/shard_map/ppermute | solution.py:130
  97.3 4.1 %shard_map.25 = f32[90,23,1024]{2,1,0:T(8,128)} custom-call(bf16[90,23,1024]{2,1,0:T(8,128)(2,1)S(1)} %bitcast.11, bf16[20,16,1024]{2,1,0:T(8,128)(2,1)S(1)} %collective-permute-done.left.refs_1_.edge_l, bf16[20,16,1024]{2,1,0:T(8,128)(2,1)S(1)} %collective-permute-done.1.right.refs_2_.edge_r, ...), custom_call_target="tpu_custom_call", output_to_operand_aliasing={{}: (7, {})} | custom-call | flops 5000000 | bytes 50000 | tf_op jit(solution)/shard_map/pallas_call | solution.py:175
  (4 shorter events, 0.0 us)
Async XLA Ops:
  0.0 2.3 %copy-start = (bf16[23,90,1024]{2,0,1:T(8,128)(2,1)S(1)}, bf16[23,90,1024]{2,0,1:T(8,128)(2,1)}, u32[]{:S(2)}) copy-start(bf16[23,90,1024]{2,0,1:T(8,128)(2,1)} %param.1) | copy-start | bytes 12718084
  2.4 17.3 %collective-permute-start = (bf16[20,16,1024]{2,1,0:T(8,128)(2,1)S(1)}, bf16[20,16,1024]{2,1,0:T(8,128)(2,1)S(1)}, u32[]{:S(2)}, u32[]{:S(2)}) collective-permute-start(bf16[20,16,1024]{2,1,0:T(8,128)(2,1)S(1)} %get-tuple-element.17), channel_id=1, source_target_pairs={{0,1},{1,2},{2,3},{3,4},{4,5},{5,6},{6,7},{7,8},{8,9},{9,10},{10,1... | collective-permute-start | bytes 1966088 | tf_op jit(solution)/shard_map/ppermute | solution.py:130
  5.1 17.0 %collective-permute-start.1 = (bf16[20,16,1024]{2,1,0:T(8,128)(2,1)S(1)}, bf16[20,16,1024]{2,1,0:T(8,128)(2,1)S(1)}, u32[]{:S(2)}, u32[]{:S(2)}) collective-permute-start(bf16[20,16,1024]{2,1,0:T(8,128)(2,1)S(1)} %get-tuple-element.18), channel_id=1, source_target_pairs={{0,15},{1,0},{2,1},{3,2},{4,3},{5,4},{6,5},{7,6},{8,7},{9,8},{10,9... | collective-permute-start | bytes 1966088 | tf_op jit(solution)/shard_map/ppermute | solution.py:130
  23.3 52.0 %collective-permute-start.4 = (f32[10,23,1024]{2,1,0:T(8,128)S(1)}, f32[10,23,1024]{2,1,0:T(8,128)S(1)}, u32[]{:S(2)}, u32[]{:S(2)}) collective-permute-start(f32[10,23,1024]{2,1,0:T(8,128)S(1)} %get-tuple-element.21), channel_id=1, source_target_pairs={{0,16},{16,32},{32,48},{48,64},{64,80},{80,96},{96,112},{112,128},... | collective-permute-start | bytes 2826248 | tf_op jit(solution)/shard_map/ppermute | solution.py:130
  25.3 52.6 %collective-permute-start.5 = (f32[10,23,1024]{2,1,0:T(8,128)S(1)}, f32[10,23,1024]{2,1,0:T(8,128)S(1)}, u32[]{:S(2)}, u32[]{:S(2)}) collective-permute-start(f32[10,23,1024]{2,1,0:T(8,128)S(1)} %get-tuple-element.22), channel_id=1, source_target_pairs={{0,240},{16,0},{32,16},{48,32},{64,48},{80,64},{96,80},{112,96},{1... | collective-permute-start | bytes 2826248 | tf_op jit(solution)/shard_map/ppermute | solution.py:130
  31.8 31.1 %collective-permute-start.10 = (bf16[70,16,256]{2,1,0:T(8,128)(2,1)S(1)}, bf16[70,16,256]{2,1,0:T(8,128)(2,1)S(1)}, u32[]{:S(2)}, u32[]{:S(2)}) collective-permute-start(bf16[70,16,256]{2,1,0:T(8,128)(2,1)S(1)} %get-tuple-element.27), channel_id=1, source_target_pairs={{0,1},{1,2},{2,3},{3,4},{4,5},{5,6},{6,7},{7,8},{8,9},{9,10},{10,1... | collective-permute-start | bytes 1720328 | tf_op jit(solution)/shard_map/ppermute | solution.py:130
  31.9 32.3 %collective-permute-start.11 = (bf16[70,16,256]{2,1,0:T(8,128)(2,1)S(1)}, bf16[70,16,256]{2,1,0:T(8,128)(2,1)S(1)}, u32[]{:S(2)}, u32[]{:S(2)}) collective-permute-start(bf16[70,16,256]{2,1,0:T(8,128)(2,1)S(1)} %get-tuple-element.28), channel_id=1, source_target_pairs={{0,15},{1,0},{2,1},{3,2},{4,3},{5,4},{6,5},{7,6},{8,7},{9,8},{10,9... | collective-permute-start | bytes 1720328 | tf_op jit(solution)/shard_map/ppermute | solution.py:130
  32.6 42.6 %collective-permute-start.8 = (bf16[70,16,256]{2,1,0:T(8,128)(2,1)S(1)}, bf16[70,16,256]{2,1,0:T(8,128)(2,1)S(1)}, u32[]{:S(2)}, u32[]{:S(2)}) collective-permute-start(bf16[70,16,256]{2,1,0:T(8,128)(2,1)S(1)} %get-tuple-element.25), channel_id=1, source_target_pairs={{0,1},{1,2},{2,3},{3,4},{4,5},{5,6},{6,7},{7,8},{8,9},{9,10},{10,1... | collective-permute-start | bytes 1720328 | tf_op jit(solution)/shard_map/ppermute | solution.py:130
  62.9 22.2 %collective-permute-start.9 = (bf16[70,16,256]{2,1,0:T(8,128)(2,1)S(1)}, bf16[70,16,256]{2,1,0:T(8,128)(2,1)S(1)}, u32[]{:S(2)}, u32[]{:S(2)}) collective-permute-start(bf16[70,16,256]{2,1,0:T(8,128)(2,1)S(1)} %get-tuple-element.26), channel_id=1, source_target_pairs={{0,15},{1,0},{2,1},{3,2},{4,3},{5,4},{6,5},{7,6},{8,7},{9,8},{10,9... | collective-permute-start | bytes 1720328 | tf_op jit(solution)/shard_map/ppermute | solution.py:130
  64.2 25.0 %collective-permute-start.6 = (bf16[70,16,256]{2,1,0:T(8,128)(2,1)S(1)}, bf16[70,16,256]{2,1,0:T(8,128)(2,1)S(1)}, u32[]{:S(2)}, u32[]{:S(2)}) collective-permute-start(bf16[70,16,256]{2,1,0:T(8,128)(2,1)S(1)} %get-tuple-element.23), channel_id=1, source_target_pairs={{0,1},{1,2},{2,3},{3,4},{4,5},{5,6},{6,7},{7,8},{8,9},{9,10},{10,1... | collective-permute-start | bytes 1720328 | tf_op jit(solution)/shard_map/ppermute | solution.py:130
  75.2 16.0 %collective-permute-start.7 = (bf16[70,16,256]{2,1,0:T(8,128)(2,1)S(1)}, bf16[70,16,256]{2,1,0:T(8,128)(2,1)S(1)}, u32[]{:S(2)}, u32[]{:S(2)}) collective-permute-start(bf16[70,16,256]{2,1,0:T(8,128)(2,1)S(1)} %get-tuple-element.24), channel_id=1, source_target_pairs={{0,15},{1,0},{2,1},{3,2},{4,3},{5,4},{6,5},{7,6},{8,7},{9,8},{10,9... | collective-permute-start | bytes 1720328 | tf_op jit(solution)/shard_map/ppermute | solution.py:130
  75.4 20.0 %collective-permute-start.2 = (bf16[70,16,256]{2,1,0:T(8,128)(2,1)S(1)}, bf16[70,16,256]{2,1,0:T(8,128)(2,1)S(1)}, u32[]{:S(2)}, u32[]{:S(2)}) collective-permute-start(bf16[70,16,256]{2,1,0:T(8,128)(2,1)S(1)} %get-tuple-element.19), channel_id=1, source_target_pairs={{0,1},{1,2},{2,3},{3,4},{4,5},{5,6},{6,7},{7,8},{8,9},{9,10},{10,1... | collective-permute-start | bytes 1720328 | tf_op jit(solution)/shard_map/ppermute | solution.py:130
  77.9 19.4 %collective-permute-start.3 = (bf16[70,16,256]{2,1,0:T(8,128)(2,1)S(1)}, bf16[70,16,256]{2,1,0:T(8,128)(2,1)S(1)}, u32[]{:S(2)}, u32[]{:S(2)}) collective-permute-start(bf16[70,16,256]{2,1,0:T(8,128)(2,1)S(1)} %get-tuple-element.20), channel_id=1, source_target_pairs={{0,15},{1,0},{2,1},{3,2},{4,3},{5,4},{6,5},{7,6},{8,7},{9,8},{10,9... | collective-permute-start | bytes 1720328 | tf_op jit(solution)/shard_map/ppermute | solution.py:130

commit v2 on v0

v2 whole, which is shorter than its diff:
```python
import functools

import jax
import jax.numpy as jnp
from jax import lax
from jax.experimental import pallas as pl
from jax.experimental.pallas import tpu as pltpu
from jax.sharding import PartitionSpec as P

DAY_HALF = 15
LON_HALF = 10
DAY_PAD = 16
DAY_WIN = 2 * DAY_HALF + 1
LON_WIN = 2 * LON_HALF + 1
SCALE = 1.0 / (DAY_WIN * LON_WIN)
BLOCK = 256
WIDTHS = (512, 256, 256)
PARTS = 2
VMEM = pl.BlockSpec(memory_space=pltpu.VMEM)
ANY = pl.BlockSpec(memory_space=pl.ANY)


def day_matrix(days, core):
    shape = (days, 2 * DAY_PAD + days)
    d = lax.broadcasted_iota(jnp.int32, shape, 0)
    col = lax.broadcasted_iota(jnp.int32, shape, 1)
    halo = col < 2 * DAY_PAD
    row = col % DAY_PAD
    from_left = (col < DAY_PAD) == (core == 0)
    s = jnp.where(halo, jnp.where(from_left, row - DAY_HALF, row + days), col - 2 * DAY_PAD)
    near = (s - d <= DAY_HALF) & (d - s <= DAY_HALF) & ((row < DAY_HALF) | ~halo)
    same = (s == d) & ~halo
    return (jnp.where(same, float(DAY_WIN), 0.0) - jnp.where(near, 1.0, 0.0)).astype(jnp.bfloat16)


def dot(a, *parts):
    return jnp.dot(a, jnp.concatenate(parts, axis=0), preferred_element_type=jnp.float32)


def is_direct(day):
    return (day % 4 == 1) | (day % 4 == 2)


def pack_kernel(groups, start, own, off, on):
    core = lax.axis_index("day") % 2
    days, width = own.shape[1], off.shape[2]
    cols = slice(start, start + width)

    def copy(late_days, early_days):
        late_days[...] = jnp.zeros_like(late_days)
        to = 0
        for first, count in groups:
            at, to = slice(to, to + count), to + count
            src = slice(first, first + count)
            late_days[at, :DAY_HALF, :] = own[src, days - DAY_HALF : days, cols]
            early_days[at, :, :] = own[src, :DAY_PAD, cols]

    @pl.when(core == 1)
    def _():
        copy(off, on)

    @pl.when(core == 0)
    def _():
        copy(on, off)


def edge_kernel(planes, field, off, on, to_right, to_left, first, second, either):
    lons, days, width = field.shape
    high = lons - LON_HALF
    day, z = lax.axis_index("day"), lax.axis_index("lon") % planes
    mat = day_matrix(days, day % 2)
    for c in range(width // BLOCK):
        cols = slice(c * BLOCK, (c + 1) * BLOCK)

        def anomaly(i):
            own = field[i if i < LON_HALF else high + i - LON_HALF, :, cols]
            return dot(mat, off[i, :, cols], on[i, :, cols], own)

        total = anomaly(0)
        to_left[0, :, cols] = total
        for j in range(1, LON_HALF):
            total = total + anomaly(j)
            to_left[j, :, cols] = total
        total = anomaly(2 * LON_HALF - 1)
        to_right[LON_HALF - 1, :, cols] = total
        for j in range(LON_HALF - 2, -1, -1):
            total = total + anomaly(LON_HALF + j)
            to_right[j, :, cols] = total

    half = width // 2

    def copy(src):
        first[...] = src[:, :, :half]
        second[...] = src[:, :, half:]

    @pl.when(z == 0)
    def _():
        copy(to_left)

    @pl.when(z != 0)
    def _():
        copy(to_right)

    either[...] = jnp.where(is_direct(day), second[...], first[...])


def main_kernel(start, own, edge_off, edge_on, mid_direct, mid_diag, mid_on, *rest):
    _, out, ends, g, buf, sems = rest
    lons, days, _ = own.shape
    width = mid_direct.shape[2]
    high = lons - LON_HALF
    day = lax.axis_index("day")
    mat = day_matrix(days, day % 2)
    direct = is_direct(day)
    step = (high - LON_HALF) // PARTS
    block = g.shape[2]

    def copies(b):
        cols = slice(start + b * block, start + (b + 1) * block)
        for k in range(PARTS):
            src = slice(k * step, (k + 1) * step)
            dst = slice(LON_HALF + k * step, LON_HALF + (k + 1) * step)
            yield pltpu.make_async_copy(buf.at[b % 2, src], out.at[dst, :, cols], sems.at[b % 2, k])

    blocks = width // block
    for b in range(blocks):
        first = start + b * block
        cols = slice(first, first + block)
        local_cols = slice(b * block, (b + 1) * block)

        for l in range(LON_HALF):
            for at, e in ((l, l), (high + l, LON_HALF + l)):
                g[at] = dot(mat, edge_off[e, :, cols], edge_on[e, :, cols], own[at, :, cols])

        def inner(i, _):
            l = LON_HALF + i
            off = jnp.where(direct, mid_direct[i, :, local_cols], mid_diag[i, :, cols])
            g[l] = dot(mat, off, mid_on[i, :, cols], own[l, :, cols])
            return 0

        lax.fori_loop(0, high - LON_HALF, inner, 0, unroll=10)
        if b >= 2:
            for copy in copies(b - 2):
                copy.wait()
        slot = buf.at[b % 2]
        moves = list(copies(b))

        total = g[0]
        for l in range(1, LON_HALF):
            total = total + g[l]
        for l in range(LON_HALF):
            total = total + g[l + LON_HALF]
            ends[l, :, local_cols] = total
        total = total + g[2 * LON_HALF]
        slot[0] = total * SCALE

        def center(l, total):
            total = total + (g[l + LON_HALF] - g[l - LON_HALF - 1])
            slot[l - LON_HALF] = total * SCALE
            return total

        at = LON_HALF + 1
        for k in range(PARTS):
            to = LON_HALF + (k + 1) * step
            total = lax.fori_loop(at, to, center, total, unroll=5)
            at = to
            moves[k].start()
        for j in range(LON_HALF):
            total = total - g[high + j - LON_HALF - 1]
            ends[LON_HALF + j, :, local_cols] = total
    for b in range(max(0, blocks - 2), blocks):
        for copy in copies(b):
            copy.wait()


def join_kernel(planes, starts, from_l, from_r, first, either, second, *rest):
    *ends, prev, out, buf, sems = rest
    high = out.shape[0] - LON_HALF
    day, z = lax.axis_index("day"), lax.axis_index("lon") % planes
    direct = is_direct(day)
    half = first.shape[2]
    moves = []
    for side, (near, plane, row) in enumerate(((from_l, 0, 0), (from_r, planes - 1, high))):
        gain = jnp.where(z == plane, 1.0, 0.0)
        for start, end in zip(starts, ends):
            for at in range(start, start + end.shape[2], BLOCK):
                cols = slice(at, at + BLOCK)
                own_cols = slice(at - start, at - start + BLOCK)
                a, b = (first, either) if at < half else (either, second)
                far_cols = slice(at % half, at % half + BLOCK)

                def add(j, _):
                    far = jnp.where(direct, a[j, :, far_cols], b[j, :, far_cols])
                    value = end[side * LON_HALF + j, :, own_cols] + near[j, :, cols] + far * gain
                    buf[side, j, :, cols] = value * SCALE
                    return 0

                lax.fori_loop(0, LON_HALF, add, 0, unroll=5)
        moves.append(pltpu.make_async_copy(buf.at[side], out.at[row : row + LON_HALF], sems.at[side]))
        moves[-1].start()
    for move in moves:
        move.wait()


def local(sizes, field):
    field = jnp.transpose(field, (1, 0, 2))
    lons, days, cols = field.shape
    high = lons - LON_HALF
    mid = high - LON_HALF
    nday, nlon = sizes
    nz = nlon // 2
    params = pltpu.CompilerParams(vmem_limit_bytes=24 * 2**20)
    starts = [sum(WIDTHS[:c]) for c in range(len(WIDTHS))]
    f32 = lambda w: jax.ShapeDtypeStruct((LON_HALF, days, w), jnp.float32)

    def cost(work):
        return pl.CostEstimate(flops=10**3 * work, bytes_accessed=10 * work, transcendentals=0)

    def swap(first, stride):
        pairs = []
        for i in range(first, nday, stride):
            pairs += [(i, (i + 1) % nday), ((i + 1) % nday, i)]
        return pairs

    def pack(groups, start, width):
        shape = (sum(n for _, n in groups), DAY_PAD, width)
        return pl.pallas_call(
            functools.partial(pack_kernel, groups, start),
            in_specs=[VMEM],
            out_specs=[VMEM] * 2,
            out_shape=[jax.ShapeDtypeStruct(shape, field.dtype)] * 2,
            cost_estimate=cost(1000),
            compiler_params=params,
        )(field)

    e_off, e_on = pack(((0, LON_HALF), (high, LON_HALF)), 0, cols)
    edge_off = lax.ppermute(e_off, "day", swap(1, 2))
    edge_on = lax.ppermute(e_on, "day", swap(0, 2))
    mid_direct = []
    for c, width in enumerate(WIDTHS):
        off, _ = pack(((LON_HALF, mid),), starts[c], width)
        mid_direct.append(lax.ppermute(off, "day", swap(1, 4)))
    off, on = pack(((LON_HALF, mid),), 0, cols)

    to_right, to_left, first, second, either = pl.pallas_call(
        functools.partial(edge_kernel, nz),
        in_specs=[VMEM] * 3,
        out_specs=[VMEM] * 5,
        out_shape=[f32(cols)] * 2 + [f32(cols // 2)] * 3,
        cost_estimate=cost(5000),
        compiler_params=params,
        name="edge",
    )(field, edge_off, edge_on)

    mid_on = lax.ppermute(on, "day", swap(0, 2))
    mid_diag = lax.ppermute(off, "day", swap(3, 4))

    at = lambda hi, zz, dd: (hi * nz + zz) * nday + dd
    last = nz - 1

    def via(planes, days_of):
        hop, land = [], []
        for hi in range(2):
            for dd in days_of:
                p = planes[dd % 4 in (1, 2)]
                for src, mid_z, dst in ((last, p, 0), (0, last - p, last)):
                    hop.append((at(hi, src, dd), at(hi, mid_z, dd ^ 3)))
                    land.append((at(hi, mid_z, dd ^ 3), at(1 - hi, dst, dd)))
        return hop, land

    all_days = range(nday)
    early = [dd for dd in all_days if dd % 4 in (0, 3)]
    late = [dd for dd in all_days if dd % 4 in (1, 2)]
    both_axes = ("lon", "day")
    hop_x, land_x = via({True: 1, False: 2}, all_days)
    hop_y, land_y = via({False: 3}, early)
    straight = []
    for hi in range(2):
        for dd in late:
            straight += [(at(hi, last, dd), at(1 - hi, 0, dd)), (at(hi, 0, dd), at(1 - hi, last, dd))]
    hopped_x = lax.ppermute(either, both_axes, hop_x)
    hopped_y = lax.ppermute(second, both_axes, hop_y)
    landed_0 = lax.ppermute(first, both_axes, straight)
    landed_x = lax.ppermute(hopped_x, both_axes, land_x)
    landed_y = lax.ppermute(hopped_y, both_axes, land_y)
    inner = [i for i in range(nlon) if i % nz != last]
    from_l = lax.ppermute(to_right, "lon", [(i, i + 1) for i in inner])
    from_r = lax.ppermute(to_left, "lon", [(i + 1, i) for i in inner])

    out, ends = None, []
    for c, width in enumerate(WIDTHS):
        args = [field, edge_off, edge_on, mid_direct[c], mid_diag, mid_on]
        specs = [VMEM] * len(args)
        body = functools.partial(main_kernel, starts[c])
        if c:
            specs.append(ANY)
            args.append(out)
            fn, alias = body, {len(args) - 1: 0}
        else:
            fn, alias = lambda *refs, body=body: body(*refs[:-5], None, *refs[-5:]), {}
        out, end = pl.pallas_call(
            fn,
            in_specs=specs,
            out_specs=[ANY, VMEM],
            out_shape=[
                jax.ShapeDtypeStruct(field.shape, jnp.float32),
                jax.ShapeDtypeStruct((2 * LON_HALF, days, width), jnp.float32),
            ],
            input_output_aliases=alias,
            scratch_shapes=[
                pltpu.VMEM((lons, days, BLOCK), jnp.float32),
                pltpu.VMEM((2, mid, days, BLOCK), jnp.float32),
                pltpu.SemaphoreType.DMA((2, PARTS)),
            ],
            cost_estimate=cost(5000),
            compiler_params=params,
        )(*args)
        ends.append(end)
    args = [from_l, from_r, landed_0, landed_x, landed_y, *ends, out]
    out = pl.pallas_call(
        functools.partial(join_kernel, nz, starts),
        in_specs=[VMEM] * (len(args) - 1) + [ANY],
        out_specs=ANY,
        out_shape=jax.ShapeDtypeStruct(field.shape, jnp.float32),
        input_output_aliases={len(args) - 1: 0},
        scratch_shapes=[
            pltpu.VMEM((2, LON_HALF, days, cols), jnp.float32),
            pltpu.SemaphoreType.DMA((2,)),
        ],
        cost_estimate=cost(3000),
        compiler_params=params,
        name="join",
    )(*args)
    return jnp.transpose(out, (1, 0, 2))


def solution(mesh):
    sizes = (mesh.shape["day"], mesh.shape["lon"])

    def body(field):
        return local(sizes, field)

    return jax.shard_map(
        body,
        mesh=mesh,
        in_specs=(P("day", "lon", None),),
        out_specs=P("day", "lon", None),
        check_vma=False,
    )
```

time: 158 us -> 115 us (0.73)
  other arithmetic: 49.6 us -> 0 us
  starting transfers between devices: 11.6 us -> 38.9 us
  waiting for transfers between devices: 81.6 us -> 56.7 us
  Pallas kernels: 0 us -> 16.5 us
  local copies, waits for them, and re-layouts: 14.4 us -> 2.25 us
    ppermute x4 -> x14, starting transfers between devices: 11.6 us -> 38.9 us  [the longest x1 8.81 us: local(): landed_0 = lax.ppermute(first, both_axes, straight)]
    ppermute x4 -> x14, waiting for transfers between devices: 81.6 us -> 56.7 us  [the longest x1 35.1 us: local(): edge_off = lax.ppermute(e_off, 'day', swap(1, 2))]
    another operation x2 -> x0, other arithmetic: 19.4 us -> none  [running(): total = jnp.cumsum(values, axis=dim)]
    pallas_call x0 -> x10, Pallas kernels: none -> 16.5 us  [the longest x3 10.9 us: local(): pl.pallas_call(fn, in_specs=specs, out_specs=[ANY, VMEM], out_shape=[jax....]
    convert_element_type x1 -> x0, other arithmetic: 13.1 us -> none  [local(): values = tall.astype(jnp.float32)]
    sub x1 -> x0, other arithmetic: 7.71 us -> none  [local(): anomaly = values[DAY_HALF:values.shape[0] - DAY_HALF] - clim]
    unnamed x9 -> x2, local copies, waits for them, and re-layouts: 9.21 us -> 2.25 us
    concatenate x1 -> x0, other arithmetic: 4.81 us -> none  [extended(): jnp.concatenate([lax.ppermute(tail, axis, [(i, (i + 1) % count) for i in...]
  transfers between devices with their start and end apart: 4 -> 14, of which waited for: 4 -> 4; matrix products, arithmetic and copies ran while one was open for 1% -> 0% of each run, Pallas kernels for 0% -> 13%
where the time goes in v2:
time: 115 us
  waiting for transfers between devices  56.7 us (49%)
  starting transfers between devices  38.9 us (34%)
  Pallas kernels  16.5 us (14%)
  local copies, waits for them, and re-layouts  2.25 us (2%)
    ppermute x1, waiting for transfers between devices, local(): edge_off = lax.ppermute(e_off, 'day', swap(1, 2))  35.1 us
    ppermute x1, waiting for transfers between devices, local(): landed_x = lax.ppermute(hopped_x, both_axes, land_x)  15.7 us
    pallas_call x3, Pallas kernels, local(): pl.pallas_call(fn, in_specs=specs, out_specs=[ANY, VMEM], out_shape=[jax....  10.9 us
    ppermute x1, starting transfers between devices, local(): landed_0 = lax.ppermute(first, both_axes, straight)  8.81 us
    ppermute x3, starting transfers between devices, local(): mid_direct.append(lax.ppermute(off, 'day', swap(1, 4)))  7.45 us
    ppermute x1, starting transfers between devices, local(): hopped_x = lax.ppermute(either, both_axes, hop_x)  6.65 us
    ppermute x1, starting transfers between devices, local(): mid_on = lax.ppermute(on, 'day', swap(0, 2))  5.89 us
    ppermute x1, waiting for transfers between devices, local(): hopped_x = lax.ppermute(either, both_axes, hop_x)  5.06 us
  transfers between devices with their start and end apart: 14, of which 4 were waited for; matrix products, arithmetic and copies ran while one was open for 0% of the time, Pallas kernels for 13%

profile of v2, /device:TPU:1, one launch (start us, length us, event | category | flops | bytes accessed | tf_op | source)
XLA Modules:
  0.0 114.6 jit_solution(4498124390625007013)
XLA Ops:
  0.0 2.3 %copy-done = bf16[23,90,1024]{2,0,1:T(8,128)(2,1)S(1)} copy-done((bf16[23,90,1024]{2,0,1:T(8,128)(2,1)S(1)}, bf16[23,90,1024]{2,0,1:T(8,128)(2,1)}, u32[]{:S(2)}) %copy-start) | copy-done | bytes 4239384
  2.3 0.3 shard_map.19
  2.6 0.8 collective-permute-start.10
  3.4 5.9 %collective-permute-start.11 = (bf16[70,16,1024]{2,1,0:T(8,128)(2,1)S(1)}, bf16[70,16,1024]{2,1,0:T(8,128)(2,1)S(1)}, u32[]{:S(2)}, u32[]{:S(2)}) collective-permute-start(bf16[70,16,1024]{2,1,0:T(8,128)(2,1)S(1)} %get-tuple-element.32), channel_id=1, source_target_pairs={{0,1},{1,0},{2,3},{3,2},{4,5},{5,4},{6,7},{7,6},{8,9},{9,8},{10,11... | collective-permute-start | bytes 6881288 | tf_op jit(solution)/shard_map/ppermute | solution.py:255
  9.3 0.1 shard_map.17
  9.4 0.1 collective-permute-start
  9.5 2.4 %collective-permute-start.1 = (bf16[20,16,1024]{2,1,0:T(8,128)(2,1)S(1)}, bf16[20,16,1024]{2,1,0:T(8,128)(2,1)S(1)}, u32[]{:S(2)}, u32[]{:S(2)}) collective-permute-start(bf16[20,16,1024]{2,1,0:T(8,128)(2,1)S(1)} %get-tuple-element.24), channel_id=1, source_target_pairs={{0,1},{1,0},{2,3},{3,2},{4,5},{5,4},{6,7},{7,6},{8,9},{9,8},{10,11... | collective-permute-start | bytes 1966088 | tf_op jit(solution)/shard_map/ppermute | solution.py:238
  11.8 0.9 shard_map.21
  12.8 1.9 %collective-permute-start.12 = (bf16[70,16,256]{2,1,0:T(8,128)(2,1)S(1)}, bf16[70,16,256]{2,1,0:T(8,128)(2,1)S(1)}, u32[]{:S(2)}, u32[]{:S(2)}) collective-permute-start(bf16[70,16,256]{2,1,0:T(8,128)(2,1)S(1)} %get-tuple-element.34), channel_id=1, source_target_pairs={{1,2},{2,1},{5,6},{6,5},{9,10},{10,9},{13,14},{14,13},{17,18},{18,... | collective-permute-start | bytes 1720328 | tf_op jit(solution)/shard_map/ppermute | solution.py:242
  14.7 0.9 shard_map.23
  15.6 35.1 %collective-permute-done.off.refs_1_.edge_off = bf16[20,16,1024]{2,1,0:T(8,128)(2,1)S(1)} collective-permute-done((bf16[20,16,1024]{2,1,0:T(8,128)(2,1)S(1)}, bf16[20,16,1024]{2,1,0:T(8,128)(2,1)S(1)}, u32[]{:S(2)}, u32[]{:S(2)}) %collective-permute-start) | collective-permute-done | bytes 655392 | tf_op jit(solution)/shard_map/ppermute | solution.py:237
  50.7 1.9 %collective-permute-start.13 = (bf16[70,16,256]{2,1,0:T(8,128)(2,1)S(1)}, bf16[70,16,256]{2,1,0:T(8,128)(2,1)S(1)}, u32[]{:S(2)}, u32[]{:S(2)}) collective-permute-start(bf16[70,16,256]{2,1,0:T(8,128)(2,1)S(1)} %get-tuple-element.37), channel_id=1, source_target_pairs={{1,2},{2,1},{5,6},{6,5},{9,10},{10,9},{13,14},{14,13},{17,18},{18,... | collective-permute-start | bytes 1720328 | tf_op jit(solution)/shard_map/ppermute | solution.py:242
  52.6 1.2 %shard_map.18 = (bf16[70,16,512]{2,1,0:T(8,128)(2,1)S(1)}, bf16[70,16,512]{2,1,0:T(8,128)(2,1)}) custom-call(bf16[90,23,1024]{2,1,0:T(8,128)(2,1)S(1)} %bitcast.6), custom_call_target="tpu_custom_call" | custom-call | flops 1000000 | bytes 10000 | tf_op jit(solution)/shard_map/pallas_call | solution.py:227
  53.8 3.6 %collective-permute-start.9 = (bf16[70,16,512]{2,1,0:T(8,128)(2,1)S(1)}, bf16[70,16,512]{2,1,0:T(8,128)(2,1)S(1)}, u32[]{:S(2)}, u32[]{:S(2)}) collective-permute-start(bf16[70,16,512]{2,1,0:T(8,128)(2,1)S(1)} %get-tuple-element.30), channel_id=1, source_target_pairs={{1,2},{2,1},{5,6},{6,5},{9,10},{10,9},{13,14},{14,13},{17,18},{18,... | collective-permute-start | bytes 3440648 | tf_op jit(solution)/shard_map/ppermute | solution.py:242
  57.4 0.6 edge.1
  58.0 0.0 collective-permute-done.12.mid_direct
  58.0 6.7 %collective-permute-start.5 = (f32[10,23,512]{2,1,0:T(8,128)S(1)}, f32[10,23,512]{2,1,0:T(8,128)S(1)}, u32[]{:S(2)}, u32[]{:S(2)}) collective-permute-start(f32[10,23,512]{2,1,0:T(8,128)S(1)} %get-tuple-element.28), channel_id=1, source_target_pairs={{112,35},{0,83},{113,18},{1,98},{114,17},{2,97},{115,32},{3,80},{1... | collective-permute-start | bytes 1413128 | tf_op jit(solution)/shard_map/ppermute | solution.py:281
  64.7 0.7 collective-permute-start.7
  65.4 5.1 %collective-permute-done.5 = f32[10,23,512]{2,1,0:T(8,128)S(1)} collective-permute-done((f32[10,23,512]{2,1,0:T(8,128)S(1)}, f32[10,23,512]{2,1,0:T(8,128)S(1)}, u32[]{:S(2)}, u32[]{:S(2)}) %collective-permute-start.5) | collective-permute-done | bytes 471072 | tf_op jit(solution)/shard_map/ppermute | solution.py:281
  70.5 2.9 %collective-permute-start.2 = (f32[10,23,1024]{2,1,0:T(8,128)S(1)}, f32[10,23,1024]{2,1,0:T(8,128)S(1)}, u32[]{:S(2)}, u32[]{:S(2)}) collective-permute-start(f32[10,23,1024]{2,1,0:T(8,128)S(1)} %get-tuple-element.25), channel_id=1, source_target_pairs={{0,16},{16,32},{32,48},{48,64},{64,80},{80,96},{96,112},{128,144},... | collective-permute-start | bytes 2826248 | tf_op jit(solution)/shard_map/ppermute | solution.py:287
  73.4 0.0 collective-permute-done.7
  73.4 1.3 %collective-permute-start.3 = (f32[10,23,1024]{2,1,0:T(8,128)S(1)}, f32[10,23,1024]{2,1,0:T(8,128)S(1)}, u32[]{:S(2)}, u32[]{:S(2)}) collective-permute-start(f32[10,23,1024]{2,1,0:T(8,128)S(1)} %get-tuple-element.26), channel_id=1, source_target_pairs={{16,0},{32,16},{48,32},{64,48},{80,64},{96,80},{112,96},{144,128},... | collective-permute-start | bytes 2826248 | tf_op jit(solution)/shard_map/ppermute | solution.py:288
  74.7 0.9 collective-permute-done.9.refs_3_
  75.6 8.8 %collective-permute-start.4 = (f32[10,23,512]{2,1,0:T(8,128)S(1)}, f32[10,23,512]{2,1,0:T(8,128)S(1)}, u32[]{:S(2)}, u32[]{:S(2)}) collective-permute-start(f32[10,23,512]{2,1,0:T(8,128)S(1)} %get-tuple-element.27), channel_id=1, source_target_pairs={{113,129},{1,241},{114,130},{2,242},{117,133},{5,245},{118,134},{6... | collective-permute-start | bytes 1413128 | tf_op jit(solution)/shard_map/ppermute | solution.py:283
  84.4 0.0 collective-permute-done.10.refs_4_.mid_diag
  84.4 1.3 %collective-permute-start.6 = (f32[10,23,512]{2,1,0:T(8,128)S(1)}, f32[10,23,512]{2,1,0:T(8,128)S(1)}, u32[]{:S(2)}, u32[]{:S(2)}) collective-permute-start(f32[10,23,512]{2,1,0:T(8,128)S(1)} %collective-permute-done.5), channel_id=1, source_target_pairs={{35,128},{83,240},{18,129},{98,241},{17,130},{97,242},{32,131},{80... | collective-permute-start | bytes 1413128 | tf_op jit(solution)/shard_map/ppermute | solution.py:284
  85.7 0.7 collective-permute-start.8
  86.4 4.9 %shard_map.20 = (f32[90,23,1024]{2,1,0:T(8,128)}, f32[20,23,512]{2,1,0:T(8,128)S(1)}) custom-call(bf16[90,23,1024]{2,1,0:T(8,128)(2,1)S(1)} %bitcast.8, bf16[20,16,1024]{2,1,0:T(8,128)(2,1)S(1)} %collective-permute-done.off.refs_1_.edge_off, bf16[20,16,1024]{2,1,0:T(8,128)(2,1)S(1)} %collective-permute-done.1.on.refs_2_.edge_on, ...), custom_call_target="tpu_custom_call" | custom-call | flops 5000000 | bytes 50000 | tf_op jit(solution)/shard_map/pallas_call | solution.py:301
  91.3 3.0 %shard_map.22 = (f32[90,23,1024]{2,1,0:T(8,128)}, f32[20,23,256]{2,1,0:T(8,128)S(1)}) custom-call(bf16[90,23,1024]{2,1,0:T(8,128)(2,1)S(1)} %bitcast.9, bf16[20,16,1024]{2,1,0:T(8,128)(2,1)S(1)} %collective-permute-done.off.refs_1_.edge_off, bf16[20,16,1024]{2,1,0:T(8,128)(2,1)S(1)} %collective-permute-done.1.on.refs_2_.edge_on, ...), custom_call_target="tpu_custom_call", output_to_operand_aliasing={{0}: (6, {})} | custom-call | flops 5000000 | bytes 50000 | tf_op jit(solution)/shard_map/pallas_call | solution.py:301
  94.3 3.0 %shard_map.24 = (f32[90,23,1024]{2,1,0:T(8,128)}, f32[20,23,256]{2,1,0:T(8,128)S(1)}) custom-call(bf16[90,23,1024]{2,1,0:T(8,128)(2,1)S(1)} %bitcast.10, bf16[20,16,1024]{2,1,0:T(8,128)(2,1)S(1)} %collective-permute-done.off.refs_1_.edge_off, bf16[20,16,1024]{2,1,0:T(8,128)(2,1)S(1)} %collective-permute-done.1.on.refs_2_.edge_on, ...), custom_call_target="tpu_custom_call", output_to_operand_aliasing={{0}: (6, {})} | custom-call | flops 5000000 | bytes 50000 | tf_op jit(solution)/shard_map/pallas_call | solution.py:301
  97.3 15.7 %collective-permute-done.6.either = f32[10,23,512]{2,1,0:T(8,128)S(1)} collective-permute-done((f32[10,23,512]{2,1,0:T(8,128)S(1)}, f32[10,23,512]{2,1,0:T(8,128)S(1)}, u32[]{:S(2)}, u32[]{:S(2)}) %collective-permute-start.6) | collective-permute-done | bytes 471072 | tf_op jit(solution)/shard_map/ppermute | solution.py:284
  113.0 1.6 %join.1 = f32[90,23,1024]{2,1,0:T(8,128)} custom-call(f32[10,23,1024]{2,1,0:T(8,128)S(1)} %collective-permute-done.2.from_l, f32[10,23,1024]{2,1,0:T(8,128)S(1)} %collective-permute-done.3.from_r, f32[10,23,512]{2,1,0:T(8,128)S(1)} %collective-permute-done.4.first, f32[10,23,512]{2,1,0:T(8,128)S(1)} %collective-permute-done.6.either, ...), custom_call_target="tpu_custom_call", output_to_operand_aliasing={{}: (8, {})} | custom-call | flops 3000000 | bytes 30000 | tf_op jit(solution)/shard_map/join/pallas_call | solution.py:320
  (8 shorter events, 0.0 us)
Async XLA Ops:
  0.0 2.3 %copy-start = (bf16[23,90,1024]{2,0,1:T(8,128)(2,1)S(1)}, bf16[23,90,1024]{2,0,1:T(8,128)(2,1)}, u32[]{:S(2)}) copy-start(bf16[23,90,1024]{2,0,1:T(8,128)(2,1)} %param.1) | copy-start | bytes 12718084
  2.6 81.8 %collective-permute-start.10 = (bf16[70,16,1024]{2,1,0:T(8,128)(2,1)S(1)}, bf16[70,16,1024]{2,1,0:T(8,128)(2,1)S(1)}, u32[]{:S(2)}, u32[]{:S(2)}) collective-permute-start(bf16[70,16,1024]{2,1,0:T(8,128)(2,1)S(1)} %get-tuple-element.31), channel_id=1, source_target_pairs={{3,4},{4,3},{7,8},{8,7},{11,12},{12,11},{15,0},{0,15},{19,20},{20,... | collective-permute-start | bytes 6881288 | tf_op jit(solution)/shard_map/ppermute | solution.py:256
  3.4 82.3 %collective-permute-start.11 = (bf16[70,16,1024]{2,1,0:T(8,128)(2,1)S(1)}, bf16[70,16,1024]{2,1,0:T(8,128)(2,1)S(1)}, u32[]{:S(2)}, u32[]{:S(2)}) collective-permute-start(bf16[70,16,1024]{2,1,0:T(8,128)(2,1)S(1)} %get-tuple-element.32), channel_id=1, source_target_pairs={{0,1},{1,0},{2,3},{3,2},{4,5},{5,4},{6,7},{7,6},{8,9},{9,8},{10,11... | collective-permute-start | bytes 6881288 | tf_op jit(solution)/shard_map/ppermute | solution.py:255
  9.4 41.3 %collective-permute-start = (bf16[20,16,1024]{2,1,0:T(8,128)(2,1)S(1)}, bf16[20,16,1024]{2,1,0:T(8,128)(2,1)S(1)}, u32[]{:S(2)}, u32[]{:S(2)}) collective-permute-start(bf16[20,16,1024]{2,1,0:T(8,128)(2,1)S(1)} %get-tuple-element.23), channel_id=1, source_target_pairs={{1,2},{2,1},{3,4},{4,3},{5,6},{6,5},{7,8},{8,7},{9,10},{10,9},{11,... | collective-permute-start | bytes 1966088 | tf_op jit(solution)/shard_map/ppermute | solution.py:237
  9.5 44.3 %collective-permute-start.1 = (bf16[20,16,1024]{2,1,0:T(8,128)(2,1)S(1)}, bf16[20,16,1024]{2,1,0:T(8,128)(2,1)S(1)}, u32[]{:S(2)}, u32[]{:S(2)}) collective-permute-start(bf16[20,16,1024]{2,1,0:T(8,128)(2,1)S(1)} %get-tuple-element.24), channel_id=1, source_target_pairs={{0,1},{1,0},{2,3},{3,2},{4,5},{5,4},{6,7},{7,6},{8,9},{9,8},{10,11... | collective-permute-start | bytes 1966088 | tf_op jit(solution)/shard_map/ppermute | solution.py:238
  12.8 45.3 %collective-permute-start.12 = (bf16[70,16,256]{2,1,0:T(8,128)(2,1)S(1)}, bf16[70,16,256]{2,1,0:T(8,128)(2,1)S(1)}, u32[]{:S(2)}, u32[]{:S(2)}) collective-permute-start(bf16[70,16,256]{2,1,0:T(8,128)(2,1)S(1)} %get-tuple-element.34), channel_id=1, source_target_pairs={{1,2},{2,1},{5,6},{6,5},{9,10},{10,9},{13,14},{14,13},{17,18},{18,... | collective-permute-start | bytes 1720328 | tf_op jit(solution)/shard_map/ppermute | solution.py:242
  50.7 14.0 %collective-permute-start.13 = (bf16[70,16,256]{2,1,0:T(8,128)(2,1)S(1)}, bf16[70,16,256]{2,1,0:T(8,128)(2,1)S(1)}, u32[]{:S(2)}, u32[]{:S(2)}) collective-permute-start(bf16[70,16,256]{2,1,0:T(8,128)(2,1)S(1)} %get-tuple-element.37), channel_id=1, source_target_pairs={{1,2},{2,1},{5,6},{6,5},{9,10},{10,9},{13,14},{14,13},{17,18},{18,... | collective-permute-start | bytes 1720328 | tf_op jit(solution)/shard_map/ppermute | solution.py:242
  53.8 21.8 %collective-permute-start.9 = (bf16[70,16,512]{2,1,0:T(8,128)(2,1)S(1)}, bf16[70,16,512]{2,1,0:T(8,128)(2,1)S(1)}, u32[]{:S(2)}, u32[]{:S(2)}) collective-permute-start(bf16[70,16,512]{2,1,0:T(8,128)(2,1)S(1)} %get-tuple-element.30), channel_id=1, source_target_pairs={{1,2},{2,1},{5,6},{6,5},{9,10},{10,9},{13,14},{14,13},{17,18},{18,... | collective-permute-start | bytes 3440648 | tf_op jit(solution)/shard_map/ppermute | solution.py:242
  58.0 12.4 %collective-permute-start.5 = (f32[10,23,512]{2,1,0:T(8,128)S(1)}, f32[10,23,512]{2,1,0:T(8,128)S(1)}, u32[]{:S(2)}, u32[]{:S(2)}) collective-permute-start(f32[10,23,512]{2,1,0:T(8,128)S(1)} %get-tuple-element.28), channel_id=1, source_target_pairs={{112,35},{0,83},{113,18},{1,98},{114,17},{2,97},{115,32},{3,80},{1... | collective-permute-start | bytes 1413128 | tf_op jit(solution)/shard_map/ppermute | solution.py:281
  64.7 8.6 %collective-permute-start.7 = (f32[10,23,512]{2,1,0:T(8,128)S(1)}, f32[10,23,512]{2,1,0:T(8,128)S(1)}, u32[]{:S(2)}, u32[]{:S(2)}) collective-permute-start(f32[10,23,512]{2,1,0:T(8,128)S(1)} %get-tuple-element.29), channel_id=1, source_target_pairs={{112,51},{0,67},{115,48},{3,64},{116,55},{4,71},{119,52},{7,68},{1... | collective-permute-start | bytes 1413128 | tf_op jit(solution)/shard_map/ppermute | solution.py:282
  70.5 42.5 %collective-permute-start.2 = (f32[10,23,1024]{2,1,0:T(8,128)S(1)}, f32[10,23,1024]{2,1,0:T(8,128)S(1)}, u32[]{:S(2)}, u32[]{:S(2)}) collective-permute-start(f32[10,23,1024]{2,1,0:T(8,128)S(1)} %get-tuple-element.25), channel_id=1, source_target_pairs={{0,16},{16,32},{32,48},{48,64},{64,80},{80,96},{96,112},{128,144},... | collective-permute-start | bytes 2826248 | tf_op jit(solution)/shard_map/ppermute | solution.py:287
  73.4 39.6 %collective-permute-start.3 = (f32[10,23,1024]{2,1,0:T(8,128)S(1)}, f32[10,23,1024]{2,1,0:T(8,128)S(1)}, u32[]{:S(2)}, u32[]{:S(2)}) collective-permute-start(f32[10,23,1024]{2,1,0:T(8,128)S(1)} %get-tuple-element.26), channel_id=1, source_target_pairs={{16,0},{32,16},{48,32},{64,48},{80,64},{96,80},{112,96},{144,128},... | collective-permute-start | bytes 2826248 | tf_op jit(solution)/shard_map/ppermute | solution.py:288
  75.6 21.7 %collective-permute-start.4 = (f32[10,23,512]{2,1,0:T(8,128)S(1)}, f32[10,23,512]{2,1,0:T(8,128)S(1)}, u32[]{:S(2)}, u32[]{:S(2)}) collective-permute-start(f32[10,23,512]{2,1,0:T(8,128)S(1)} %get-tuple-element.27), channel_id=1, source_target_pairs={{113,129},{1,241},{114,130},{2,242},{117,133},{5,245},{118,134},{6... | collective-permute-start | bytes 1413128 | tf_op jit(solution)/shard_map/ppermute | solution.py:283
  84.4 28.6 %collective-permute-start.6 = (f32[10,23,512]{2,1,0:T(8,128)S(1)}, f32[10,23,512]{2,1,0:T(8,128)S(1)}, u32[]{:S(2)}, u32[]{:S(2)}) collective-permute-start(f32[10,23,512]{2,1,0:T(8,128)S(1)} %collective-permute-done.5), channel_id=1, source_target_pairs={{35,128},{83,240},{18,129},{98,241},{17,130},{97,242},{32,131},{80... | collective-permute-start | bytes 1413128 | tf_op jit(solution)/shard_map/ppermute | solution.py:284
  85.7 27.3 %collective-permute-start.8 = (f32[10,23,512]{2,1,0:T(8,128)S(1)}, f32[10,23,512]{2,1,0:T(8,128)S(1)}, u32[]{:S(2)}, u32[]{:S(2)}) collective-permute-start(f32[10,23,512]{2,1,0:T(8,128)S(1)} %collective-permute-done.7), channel_id=1, source_target_pairs={{51,128},{67,240},{48,131},{64,243},{55,132},{71,244},{52,135},{68... | collective-permute-start | bytes 1413128 | tf_op jit(solution)/shard_map/ppermute | solution.py:285

commit v3 on v2

v3 whole, which is shorter than its diff:
```python
import functools

import jax
import jax.numpy as jnp
from jax import lax
from jax.experimental import pallas as pl
from jax.experimental.pallas import tpu as pltpu
from jax.sharding import PartitionSpec as P

DAY_HALF = 15
LON_HALF = 10
DAY_PAD = 16
DAY_WIN = 2 * DAY_HALF + 1
LON_WIN = 2 * LON_HALF + 1
SCALE = 1.0 / (DAY_WIN * LON_WIN)
BLOCK = 256
WIDTHS = (512, 256, 128, 128)
AHEAD = 2
VMEM = pl.BlockSpec(memory_space=pltpu.VMEM)
ANY = pl.BlockSpec(memory_space=pl.ANY)


def window_weights(d, s, valid):
    return jnp.where((s - d <= DAY_HALF) & (d - s <= DAY_HALF) & valid, -1.0, 0.0)


def halo_day(row, days, from_left):
    return jnp.where(from_left, row - DAY_HALF, row + days)


def off_matrix(days, core):
    d = lax.broadcasted_iota(jnp.int32, (days, DAY_PAD), 0)
    row = lax.broadcasted_iota(jnp.int32, (days, DAY_PAD), 1)
    return window_weights(d, halo_day(row, days, core == 0), row < DAY_HALF).astype(jnp.bfloat16)


def spread_matrix(days, core):
    shape = (days, DAY_HALF * DAY_PAD)
    d = lax.broadcasted_iota(jnp.int32, shape, 0)
    col = lax.broadcasted_iota(jnp.int32, shape, 1)
    s = halo_day(col // DAY_PAD, days, core == 0)
    return window_weights(d, s, col % DAY_PAD == DAY_HALF).astype(jnp.bfloat16)


def rest_matrix(days, core):
    shape = (days, DAY_PAD + days)
    d = lax.broadcasted_iota(jnp.int32, shape, 0)
    col = lax.broadcasted_iota(jnp.int32, shape, 1)
    halo = col < DAY_PAD
    s = jnp.where(halo, halo_day(col, days, core == 1), col - DAY_PAD)
    same = jnp.where((s == d) & ~halo, float(DAY_WIN), 0.0)
    return (same + window_weights(d, s, ~halo | (col < DAY_HALF))).astype(jnp.bfloat16)


def dot(a, *parts):
    b = parts[0] if len(parts) == 1 else jnp.concatenate(parts, axis=0)
    return jnp.dot(a, b, preferred_element_type=jnp.float32)


def dense_tiles(lons):
    return -(-lons * DAY_HALF // DAY_PAD)


def is_direct(day):
    return (day % 4 == 1) | (day % 4 == 2)


def pack_dense(src, base, lons, low, cols, to):
    tiles = dense_tiles(lons)
    width = cols.stop - cols.start
    full = lons - tiles

    def rows(i):
        return src[base + i, low : low + DAY_HALF, cols].astype(jnp.float32)

    def store(i, last):
        to[i] = jnp.concatenate([rows(i), last], axis=0).astype(to.dtype)

    def group(q, _):
        extra = rows(tiles + q)
        for r in range(DAY_HALF):
            store(q * DAY_HALF + r, extra[r : r + 1])
        return 0

    lax.fori_loop(0, full, group, 0)
    for i in range(full * DAY_HALF, tiles):
        store(i, jnp.zeros((1, width), jnp.float32))


def pack_plain(src, base, lons, low, cols, to):
    width = cols.stop - cols.start

    def store(i, _):
        rows = src[base + i, low : low + DAY_HALF, cols].astype(jnp.float32)
        to[i] = jnp.concatenate([rows, jnp.zeros((1, width), jnp.float32)], axis=0).astype(to.dtype)
        return 0

    lax.fori_loop(0, lons, store, 0, unroll=5)


def by_core(core, days, run):
    @pl.when(core == 1)
    def _():
        run(days - DAY_HALF, 0)

    @pl.when(core == 0)
    def _():
        run(0, days - DAY_HALF)


def pack_edge_kernel(own, off, on):
    lons, days, width = own.shape
    cols = slice(0, width)

    def run(off_low, on_low):
        pack_dense(own, 0, lons, off_low, cols, off)
        pack_plain(own, 0, lons, on_low, cols, on)

    by_core(lax.axis_index("day") % 2, days, run)


def pack_off_kernel(start, wanted, own, off):
    lons, days, _ = own.shape
    day = lax.axis_index("day")
    cols = slice(start, start + off.shape[2])

    @pl.when(is_direct(day) == wanted)
    def _():
        def run(off_low, _):
            pack_dense(own, LON_HALF, lons - 2 * LON_HALF, off_low, cols, off)

        by_core(day % 2, days, run)


def pack_on_kernel(own, on):
    lons, days, width = own.shape

    def run(_, on_low):
        pack_plain(own, LON_HALF, lons - 2 * LON_HALF, on_low, slice(0, width), on)

    by_core(lax.axis_index("day") % 2, days, run)


def edge_part(days, core, off, cols):
    tiles = off.shape[0]
    tile_mat, spread_mat = off_matrix(days, core), spread_matrix(days, core)

    def part(i):
        if i < tiles:
            return dot(tile_mat, off[i, :, cols])
        first = (i - tiles) * DAY_HALF
        rows = off[first : first + DAY_HALF, :, cols]
        return dot(spread_mat, rows.reshape(DAY_HALF * DAY_PAD, rows.shape[2]))

    return part


def edge_kernel(planes, field, off, on, to_right, to_left, first, second):
    lons, days, width = field.shape
    high = lons - LON_HALF
    day, z = lax.axis_index("day"), lax.axis_index("lon") % planes
    mat = rest_matrix(days, day % 2)
    for c in range(width // BLOCK):
        cols = slice(c * BLOCK, (c + 1) * BLOCK)
        part = edge_part(days, day % 2, off, cols)

        def anomaly(i):
            own = field[i if i < LON_HALF else high + i - LON_HALF, :, cols]
            return dot(mat, on[i, :, cols], own) + part(i)

        total = anomaly(0)
        to_left[0, :, cols] = total
        for j in range(1, LON_HALF):
            total = total + anomaly(j)
            to_left[j, :, cols] = total
        total = anomaly(2 * LON_HALF - 1)
        to_right[LON_HALF - 1, :, cols] = total
        for j in range(LON_HALF - 2, -1, -1):
            total = total + anomaly(LON_HALF + j)
            to_right[j, :, cols] = total

    half = width // 2

    def copy(src):
        first[...] = src[:, :, :half]
        second[...] = src[:, :, half:]

    @pl.when(z == 0)
    def _():
        copy(to_left)

    @pl.when(z != 0)
    def _():
        copy(to_right)


def pre_kernel(field, edge_off, edge_on, mid_on, pre):
    lons, days, width = field.shape
    high = lons - LON_HALF
    core = lax.axis_index("day") % 2
    mat = rest_matrix(days, core)
    for c in range(width // BLOCK):
        cols = slice(c * BLOCK, (c + 1) * BLOCK)
        part = edge_part(days, core, edge_off, cols)
        for i in range(2 * LON_HALF):
            l = i if i < LON_HALF else high + i - LON_HALF
            pre[l, :, cols] = dot(mat, edge_on[i, :, cols], field[l, :, cols]) + part(i)

        def inner(i, _):
            l = LON_HALF + i
            pre[l, :, cols] = dot(mat, mid_on[i, :, cols], field[l, :, cols])
            return 0

        lax.fori_loop(0, high - LON_HALF, inner, 0, unroll=10)


def far_value(direct, far, j, start, width):
    half = far[0].shape[2]
    a, b = far[:2] if start < half else far[2:]
    cols = slice(start % half, start % half + width)
    return jnp.where(direct, a[j, :, cols], b[j, :, cols])


def main_kernel(planes, start, joined, pre, mid_direct, mid_diag, *rest):
    lon_args, moving = None, []
    if joined:
        lon_args, done, (prev, out, g, buf, sems, *spare) = rest[:6], rest[6 : 6 + len(joined)], rest[6 + len(joined) :]
        moving = start_join(planes, joined, lon_args, done, out, *spare)
    elif planes:
        *lon_args, prev, out, g, buf, sems = rest
    else:
        prev, out, ends, g, buf, sems = rest
    lons, days, _ = pre.shape
    width = mid_direct.shape[2]
    high = lons - LON_HALF
    mid = high - LON_HALF
    tiles = mid_direct.shape[0]
    day = lax.axis_index("day")
    direct = is_direct(day)
    tile_mat, spread_mat = off_matrix(days, day % 2), spread_matrix(days, day % 2)
    block = g.shape[2]
    base = (lons - buf.shape[1]) // 2
    parts = sems.shape[1]
    step = buf.shape[1] // parts
    if planes:
        z = lax.axis_index("lon") % planes
        gains = jnp.where(z == 0, 1.0, 0.0), jnp.where(z == planes - 1, 1.0, 0.0)

    def copies(b):
        cols = slice(start + b * block, start + (b + 1) * block)
        for k in range(parts):
            src = slice(k * step, (k + 1) * step)
            dst = slice(base + k * step, base + (k + 1) * step)
            yield pltpu.make_async_copy(buf.at[b % 2, src], out.at[dst, :, cols], sems.at[b % 2, k])

    blocks = width // block
    for b in range(blocks):
        first = start + b * block
        cols = slice(first, first + block)
        local_cols = slice(b * block, (b + 1) * block)

        for j in range(LON_HALF):
            g[j] = pre[j, :, cols]
            g[high + j] = pre[high + j, :, cols]

        def inner(i, _):
            off = jnp.where(direct, mid_direct[i, :, local_cols], mid_diag[i, :, cols])
            g[LON_HALF + i] = pre[LON_HALF + i, :, cols] + dot(tile_mat, off)
            return 0

        lax.fori_loop(0, tiles, inner, 0, unroll=11)
        for q in range(mid - tiles):
            at = slice(q * DAY_HALF, (q + 1) * DAY_HALF)
            off = jnp.where(direct, mid_direct[at, :, local_cols], mid_diag[at, :, cols])
            l = LON_HALF + tiles + q
            g[l] = pre[l, :, cols] + dot(spread_mat, off.reshape(DAY_HALF * DAY_PAD, block))
        if b >= 2:
            for copy in copies(b - 2):
                copy.wait()
        slot = buf.at[b % 2]
        moves = list(copies(b))

        def end(side, j, total):
            if not planes:
                ends[side * LON_HALF + j, :, local_cols] = total
                return
            near = lon_args[side][j, :, cols]
            far = far_value(direct, lon_args[2:], j, first, block)
            slot[(high if side else 0) + j] = (total + near + far * gains[side]) * SCALE

        total = g[0]
        for l in range(1, LON_HALF):
            total = total + g[l]
        for l in range(LON_HALF):
            total = total + g[l + LON_HALF]
            end(0, l, total)
        total = total + g[2 * LON_HALF]
        slot[LON_HALF - base] = total * SCALE

        def center(l, total):
            total = total + (g[l + LON_HALF] - g[l - LON_HALF - 1])
            slot[l - base] = total * SCALE
            return total

        at = LON_HALF + 1
        for k in range(parts):
            to = min(base + (k + 1) * step, high)
            total = lax.fori_loop(at, to, center, total, unroll=5)
            at = to
            if k < parts - 1 or not planes:
                moves[k].start()
        for j in range(LON_HALF):
            total = total - g[high + j - LON_HALF - 1]
            end(1, j, total)
        if planes:
            moves[-1].start()
    for b in range(max(0, blocks - 2), blocks):
        for copy in copies(b):
            copy.wait()
    for move in moving:
        move.wait()


def start_join(planes, starts, lon_args, ends, out, buf, sems):
    from_l, from_r, *far_args = lon_args
    width = buf.shape[3]
    high = out.shape[0] - LON_HALF
    day, z = lax.axis_index("day"), lax.axis_index("lon") % planes
    direct = is_direct(day)
    moves = []
    for side, (near, plane, row) in enumerate(((from_l, 0, 0), (from_r, planes - 1, high))):
        gain = jnp.where(z == plane, 1.0, 0.0)
        for start, end in zip(starts, ends):
            block = min(BLOCK, end.shape[2])
            for at in range(start, start + end.shape[2], block):
                cols = slice(at, at + block)
                own_cols = slice(at - start, at - start + block)

                def add(j, _):
                    far = far_value(direct, far_args, j, at, block)
                    value = end[side * LON_HALF + j, :, own_cols] + near[j, :, cols] + far * gain
                    buf[side, j, :, cols] = value * SCALE
                    return 0

                lax.fori_loop(0, LON_HALF, add, 0, unroll=5)
        moves.append(pltpu.make_async_copy(buf.at[side], out.at[row : row + LON_HALF, :, :width], sems.at[side]))
        moves[-1].start()
    return moves


def local(sizes, field):
    field = jnp.transpose(field, (1, 0, 2))
    lons, days, cols = field.shape
    mid = lons - 2 * LON_HALF
    nday, nlon = sizes
    nz = nlon // 2
    params = pltpu.CompilerParams(vmem_limit_bytes=12 * 2**20)
    starts = [sum(WIDTHS[:c]) for c in range(len(WIDTHS))]
    f32 = lambda w: jax.ShapeDtypeStruct((LON_HALF, days, w), jnp.float32)
    bf16 = lambda *shape: jax.ShapeDtypeStruct(shape, field.dtype)

    def cost(work):
        return pl.CostEstimate(flops=10**3 * work, bytes_accessed=10 * work, transcendentals=0)

    def swap(first, stride):
        pairs = []
        for i in range(first, nday, stride):
            pairs += [(i, (i + 1) % nday), ((i + 1) % nday, i)]
        return pairs

    def call(body, args, out, work=1000):
        return pl.pallas_call(
            body,
            in_specs=[VMEM] * len(args),
            out_specs=[VMEM] * len(out) if isinstance(out, list) else VMEM,
            out_shape=out,
            cost_estimate=cost(work),
            compiler_params=params,
        )(*args)

    ends_own = jnp.concatenate([field[:LON_HALF], field[lons - LON_HALF :]], axis=0)
    shapes = [bf16(dense_tiles(2 * LON_HALF), DAY_PAD, cols), bf16(2 * LON_HALF, DAY_PAD, cols)]
    e_off, e_on = call(pack_edge_kernel, [ends_own], shapes)
    edge_off = lax.ppermute(e_off, "day", swap(1, 2))
    edge_on = lax.ppermute(e_on, "day", swap(0, 2))

    mid_direct = []
    for c, width in enumerate(WIDTHS):
        off = call(functools.partial(pack_off_kernel, starts[c], True), [field], bf16(dense_tiles(mid), DAY_PAD, width))
        mid_direct.append(lax.ppermute(off, "day", swap(1, 4)))
    on = call(pack_on_kernel, [field], bf16(mid, DAY_PAD, cols))
    off = call(functools.partial(pack_off_kernel, 0, False), [field], bf16(dense_tiles(mid), DAY_PAD, cols))

    to_right, to_left, first, second = pl.pallas_call(
        functools.partial(edge_kernel, nz),
        in_specs=[VMEM] * 3,
        out_specs=[VMEM] * 4,
        out_shape=[f32(cols)] * 2 + [f32(cols // 2)] * 2,
        cost_estimate=cost(5000),
        compiler_params=params,
        name="edge",
    )(field, edge_off, edge_on)

    mid_on = lax.ppermute(on, "day", swap(0, 2))
    mid_diag = lax.ppermute(off, "day", swap(3, 4))

    at = lambda hi, zz, dd: (hi * nz + zz) * nday + dd
    last = nz - 1

    def via(p, days_of):
        hop, land = [], []
        for hi in range(2):
            for dd in days_of:
                for src, mid_z, dst in ((last, p, 0), (0, last - p, last)):
                    hop.append((at(hi, src, dd), at(hi, mid_z, dd ^ 3)))
                    land.append((at(hi, mid_z, dd ^ 3), at(1 - hi, dst, dd)))
        return hop, land

    diag_days = [dd for dd in range(nday) if dd % 4 in (0, 3)]
    direct_days = [dd for dd in range(nday) if dd % 4 in (1, 2)]
    both_axes = ("lon", "day")
    straight = []
    for hi in range(2):
        for dd in direct_days:
            straight += [(at(hi, last, dd), at(1 - hi, 0, dd)), (at(hi, 0, dd), at(1 - hi, last, dd))]
    landed = []
    for x, p, days_of in ((first, 2, diag_days), (second, 1, direct_days), (second, 3, diag_days)):
        hop, land = via(p, days_of)
        hopped = lax.ppermute(x, both_axes, hop)
        landed.append(lax.ppermute(hopped, both_axes, land))
    landed.insert(0, lax.ppermute(first, both_axes, straight))
    inner = [i for i in range(nlon) if i % nz != last]
    from_l = lax.ppermute(to_right, "lon", [(i, i + 1) for i in inner])
    from_r = lax.ppermute(to_left, "lon", [(i + 1, i) for i in inner])

    pre = call(pre_kernel, [field, edge_off, edge_on, mid_on], jax.ShapeDtypeStruct(field.shape, jnp.float32), work=9000)
    lon_args = [from_l, from_r, *landed]
    whole = jax.ShapeDtypeStruct(field.shape, jnp.float32)
    out, ends = None, []
    for c, width in enumerate(WIDTHS):
        own_join = c >= AHEAD
        joined = starts[:AHEAD] if c == AHEAD else []
        block = min(BLOCK, width)
        args = [pre, mid_direct[c], mid_diag] + (lon_args if own_join else []) + (ends if joined else [])
        specs = [VMEM] * len(args)
        body = functools.partial(main_kernel, nz if own_join else 0, starts[c], joined)
        if c:
            specs.append(ANY)
            args.append(out)
            fn, alias = body, {len(args) - 1: 0}
        else:
            fn, alias = lambda *refs, body=body: body(*refs[:-5], None, *refs[-5:]), {}
        slots = min(2, width // block)
        scratch = [
            pltpu.VMEM((lons, days, block), jnp.float32),
            pltpu.VMEM((slots, lons if own_join else mid, days, block), jnp.float32),
            pltpu.SemaphoreType.DMA((slots, 3 if own_join else 2)),
        ]
        if joined:
            scratch += [pltpu.VMEM((2, LON_HALF, days, starts[c]), jnp.float32), pltpu.SemaphoreType.DMA((2,))]
        tail = jax.ShapeDtypeStruct((2 * LON_HALF, days, width), jnp.float32)
        res = pl.pallas_call(
            fn,
            in_specs=specs,
            out_specs=[ANY] if own_join else [ANY, VMEM],
            out_shape=[whole] if own_join else [whole, tail],
            input_output_aliases=alias,
            scratch_shapes=scratch,
            cost_estimate=cost(5000),
            compiler_params=params,
        )(*args)
        out = res[0]
        ends += res[1:]
    return jnp.transpose(out, (1, 0, 2))


def solution(mesh):
    sizes = (mesh.shape["day"], mesh.shape["lon"])

    def body(field):
        return local(sizes, field)

    return jax.shard_map(
        body,
        mesh=mesh,
        in_specs=(P("day", "lon", None),),
        out_specs=P("day", "lon", None),
        check_vma=False,
    )
```

time: 115 us -> 114 us (level)
  waiting for transfers between devices: 56.7 us -> 48.9 us
  starting transfers between devices: 38.9 us -> 42.9 us
  Pallas kernels: 16.5 us -> 20.3 us
    ppermute x5 -> x7, waiting for transfers between devices: 20.7 us -> 12.2 us  [the longest x1 6.87 us: local(): landed.insert(0, lax.ppermute(first, both_axes, straight))]
    ppermute x3 -> x4, waiting for transfers between devices: 0.89 us -> 8.11 us  [local(): mid_direct.append(lax.ppermute(off, 'day', swap(1, 4)))]
    ppermute x1, waiting for transfers between devices: 35.1 us -> 28.5 us  [local(): edge_off = lax.ppermute(e_off, 'day', swap(1, 2))]
    ppermute x1, starting transfers between devices: 5.89 us -> 0.12 us  [local(): mid_on = lax.ppermute(on, 'day', swap(0, 2))]
    ppermute x3 -> x4, starting transfers between devices: 7.45 us -> 11.1 us  [local(): mid_direct.append(lax.ppermute(off, 'day', swap(1, 4)))]
    pallas_call x9 -> x12, Pallas kernels: 15.9 us -> 19.4 us  [the longest x4 12.1 us: local(): pl.pallas_call(fn, in_specs=specs, out_specs=[ANY] if own_join else [ANY,...]
    ppermute x1, starting transfers between devices: 2.36 us -> 5.86 us  [local(): edge_on = lax.ppermute(e_on, 'day', swap(0, 2))]
    ppermute x1, starting transfers between devices: 0.09 us -> 2.76 us  [local(): edge_off = lax.ppermute(e_off, 'day', swap(1, 2))]
  transfers between devices with their start and end apart: 14 -> 17, of which waited for: 4 -> 5; matrix products, arithmetic and copies ran while one was open for 0% -> 0% of each run, Pallas kernels for 13% -> 16%
where the time goes in v3:
time: 114 us
  waiting for transfers between devices  48.9 us (43%)
  starting transfers between devices  42.9 us (38%)
  Pallas kernels  20.3 us (18%)
  local copies, waits for them, and re-layouts  1.4 us (1%)
    ppermute x1, waiting for transfers between devices, local(): edge_off = lax.ppermute(e_off, 'day', swap(1, 2))  28.5 us
    pallas_call x4, Pallas kernels, local(): pl.pallas_call(fn, in_specs=specs, out_specs=[ANY] if own_join else [ANY,...  12.1 us
    ppermute x4, starting transfers between devices, local(): mid_direct.append(lax.ppermute(off, 'day', swap(1, 4)))  11.1 us
    ppermute x3, starting transfers between devices, local(): hopped = lax.ppermute(x, both_axes, hop)  10.5 us
    ppermute x4, waiting for transfers between devices, local(): mid_direct.append(lax.ppermute(off, 'day', swap(1, 4)))  8.11 us
    pallas_call x8, Pallas kernels, call(): pl.pallas_call(body, in_specs=[VMEM] * len(args), out_specs=[VMEM] * len(...  7.25 us
    ppermute x1, waiting for transfers between devices, local(): landed.insert(0, lax.ppermute(first, both_axes, straight))  6.87 us
    ppermute x1, starting transfers between devices, local(): edge_on = lax.ppermute(e_on, 'day', swap(0, 2))  5.86 us
  transfers between devices with their start and end apart: 17, of which 5 were waited for; matrix products, arithmetic and copies ran while one was open for 0% of the time, Pallas kernels for 16%

profile of v3, /device:TPU:1, one launch (start us, length us, event | category | flops | bytes accessed | tf_op | source)
XLA Modules:
  0.0 114.0 jit_solution(1469653362627804748)
XLA Ops:
  0.0 1.4 %fusion = (bf16[10,23,1024]{2,1,0:T(8,128)(2,1)S(1)}, bf16[10,23,1024]{2,1,0:T(8,128)(2,1)S(1)}) fusion(bf16[90,23,1024]{2,1,0:T(8,128)(2,1)} %bitcast.2), kind=kLoop, calls=%fused_computation.1 | loop fusion | bytes 1884160 | tf_op jit(solution)/shard_map/slice | solution.py:381
  1.5 0.2 shard_map.17
  1.7 2.8 %collective-permute-start = (bf16[19,16,1024]{2,1,0:T(8,128)(2,1)S(1)}, bf16[19,16,1024]{2,1,0:T(8,128)(2,1)S(1)}, u32[]{:S(2)}, u32[]{:S(2)}) collective-permute-start(bf16[19,16,1024]{2,1,0:T(8,128)(2,1)S(1)} %get-tuple-element.15), channel_id=1, source_target_pairs={{1,2},{2,1},{3,4},{4,3},{5,6},{6,5},{7,8},{8,7},{9,10},{10,9},{11,... | collective-permute-start | bytes 1867784 | tf_op jit(solution)/shard_map/ppermute | solution.py:384
  4.5 0.8 collective-permute-start.4
  5.2 5.9 %collective-permute-start.1 = (bf16[20,16,1024]{2,1,0:T(8,128)(2,1)S(1)}, bf16[20,16,1024]{2,1,0:T(8,128)(2,1)S(1)}, u32[]{:S(2)}, u32[]{:S(2)}) collective-permute-start(bf16[20,16,1024]{2,1,0:T(8,128)(2,1)S(1)} %get-tuple-element.16), channel_id=1, source_target_pairs={{0,1},{1,0},{2,3},{3,2},{4,5},{5,4},{6,7},{7,6},{8,9},{9,8},{10,11... | collective-permute-start | bytes 1966088 | tf_op jit(solution)/shard_map/ppermute | solution.py:385
  11.1 0.3 shard_map.18
  11.5 0.1 shard_map.23
  11.6 1.9 %collective-permute-start.15 = (bf16[66,16,512]{2,1,0:T(8,128)(2,1)S(1)}, bf16[66,16,512]{2,1,0:T(8,128)(2,1)S(1)}, u32[]{:S(2)}, u32[]{:S(2)}) collective-permute-start(bf16[66,16,512]{2,1,0:T(8,128)(2,1)S(1)} %shard_map.23), channel_id=1, source_target_pairs={{1,2},{2,1},{5,6},{6,5},{9,10},{10,9},{13,14},{14,13},{17,18},{18,... | collective-permute-start | bytes 3244040 | tf_op jit(solution)/shard_map/ppermute | solution.py:390
  13.7 28.5 %collective-permute-done.edge_off.off = bf16[19,16,1024]{2,1,0:T(8,128)(2,1)S(1)} collective-permute-done((bf16[19,16,1024]{2,1,0:T(8,128)(2,1)S(1)}, bf16[19,16,1024]{2,1,0:T(8,128)(2,1)S(1)}, u32[]{:S(2)}, u32[]{:S(2)}) %collective-permute-start) | collective-permute-done | bytes 622624 | tf_op jit(solution)/shard_map/ppermute | solution.py:384
  42.2 3.6 %collective-permute-start.14 = (bf16[66,16,128]{2,1,0:T(8,128)(2,1)S(1)}, bf16[66,16,128]{2,1,0:T(8,128)(2,1)S(1)}, u32[]{:S(2)}, u32[]{:S(2)}) collective-permute-start(bf16[66,16,128]{2,1,0:T(8,128)(2,1)S(1)} %shard_map.22), channel_id=1, source_target_pairs={{1,2},{2,1},{5,6},{6,5},{9,10},{10,9},{13,14},{14,13},{17,18},{18,... | collective-permute-start | bytes 811016 | tf_op jit(solution)/shard_map/ppermute | solution.py:390
  45.9 0.1 shard_map.25
  46.0 1.9 %collective-permute-start.16 = (bf16[66,16,256]{2,1,0:T(8,128)(2,1)S(1)}, bf16[66,16,256]{2,1,0:T(8,128)(2,1)S(1)}, u32[]{:S(2)}, u32[]{:S(2)}) collective-permute-start(bf16[66,16,256]{2,1,0:T(8,128)(2,1)S(1)} %shard_map.25), channel_id=1, source_target_pairs={{1,2},{2,1},{5,6},{6,5},{9,10},{10,9},{13,14},{14,13},{17,18},{18,... | collective-permute-start | bytes 1622024 | tf_op jit(solution)/shard_map/ppermute | solution.py:390
  47.9 1.0 edge.1
  48.9 8.1 %collective-permute-done.14.mid_direct = bf16[66,16,128]{2,1,0:T(8,128)(2,1)S(1)} collective-permute-done((bf16[66,16,128]{2,1,0:T(8,128)(2,1)S(1)}, bf16[66,16,128]{2,1,0:T(8,128)(2,1)S(1)}, u32[]{:S(2)}, u32[]{:S(2)}) %collective-permute-start.14) | collective-permute-done | bytes 270368 | tf_op jit(solution)/shard_map/ppermute | solution.py:390
  57.0 9.1 %collective-permute-start.10 = (f32[10,23,512]{2,1,0:T(8,128)S(1)}, f32[10,23,512]{2,1,0:T(8,128)S(1)}, u32[]{:S(2)}, u32[]{:S(2)}) collective-permute-start(f32[10,23,512]{2,1,0:T(8,128)S(1)} %get-tuple-element.20), channel_id=1, source_target_pairs={{113,18},{1,98},{114,17},{2,97},{117,22},{5,102},{118,21},{6,101},... | collective-permute-start | bytes 1413128 | tf_op jit(solution)/shard_map/ppermute | solution.py:429
  66.1 0.7 collective-permute-start.12
  66.8 0.7 collective-permute-start.8
  67.5 4.3 %collective-permute-done.10 = f32[10,23,512]{2,1,0:T(8,128)S(1)} collective-permute-done((f32[10,23,512]{2,1,0:T(8,128)S(1)}, f32[10,23,512]{2,1,0:T(8,128)S(1)}, u32[]{:S(2)}, u32[]{:S(2)}) %collective-permute-start.10) | collective-permute-done | bytes 471072 | tf_op jit(solution)/shard_map/ppermute | solution.py:429
  71.8 2.4 %collective-permute-start.7 = (f32[10,23,512]{2,1,0:T(8,128)S(1)}, f32[10,23,512]{2,1,0:T(8,128)S(1)}, u32[]{:S(2)}, u32[]{:S(2)}) collective-permute-start(f32[10,23,512]{2,1,0:T(8,128)S(1)} %get-tuple-element.19), channel_id=1, source_target_pairs={{113,129},{1,241},{114,130},{2,242},{117,133},{5,245},{118,134},{6... | collective-permute-start | bytes 1413128 | tf_op jit(solution)/shard_map/ppermute | solution.py:431
  74.2 1.3 %collective-permute-start.11 = (f32[10,23,512]{2,1,0:T(8,128)S(1)}, f32[10,23,512]{2,1,0:T(8,128)S(1)}, u32[]{:S(2)}, u32[]{:S(2)}) collective-permute-start(f32[10,23,512]{2,1,0:T(8,128)S(1)} %collective-permute-done.10), channel_id=1, source_target_pairs={{18,129},{98,241},{17,130},{97,242},{22,133},{102,245},{21,134},{1... | collective-permute-start | bytes 1413128 | tf_op jit(solution)/shard_map/ppermute | solution.py:430
  75.5 5.5 %collective-permute-start.5 = (f32[10,23,1024]{2,1,0:T(8,128)S(1)}, f32[10,23,1024]{2,1,0:T(8,128)S(1)}, u32[]{:S(2)}, u32[]{:S(2)}) collective-permute-start(f32[10,23,1024]{2,1,0:T(8,128)S(1)} %get-tuple-element.17), channel_id=1, source_target_pairs={{0,16},{16,32},{32,48},{48,64},{64,80},{80,96},{96,112},{128,144},... | collective-permute-start | bytes 2826248 | tf_op jit(solution)/shard_map/ppermute | solution.py:433
  81.1 6.9 %collective-permute-done.7.rest_2_ = f32[10,23,512]{2,1,0:T(8,128)S(1)} collective-permute-done((f32[10,23,512]{2,1,0:T(8,128)S(1)}, f32[10,23,512]{2,1,0:T(8,128)S(1)}, u32[]{:S(2)}, u32[]{:S(2)}) %collective-permute-start.7) | collective-permute-done | bytes 471072 | tf_op jit(solution)/shard_map/ppermute | solution.py:431
  87.9 1.3 %collective-permute-start.6 = (f32[10,23,1024]{2,1,0:T(8,128)S(1)}, f32[10,23,1024]{2,1,0:T(8,128)S(1)}, u32[]{:S(2)}, u32[]{:S(2)}) collective-permute-start(f32[10,23,1024]{2,1,0:T(8,128)S(1)} %get-tuple-element.18), channel_id=1, source_target_pairs={{16,0},{32,16},{48,32},{64,48},{80,64},{96,80},{112,96},{144,128},... | collective-permute-start | bytes 2826248 | tf_op jit(solution)/shard_map/ppermute | solution.py:434
  89.2 1.0 collective-permute-done.11.rest_4_
  90.3 0.7 collective-permute-start.13
  91.0 0.7 collective-permute-start.9
  91.8 3.6 %collective-permute-start.3 = (bf16[66,16,128]{2,1,0:T(8,128)(2,1)S(1)}, bf16[66,16,128]{2,1,0:T(8,128)(2,1)S(1)}, u32[]{:S(2)}, u32[]{:S(2)}) collective-permute-start(bf16[66,16,128]{2,1,0:T(8,128)(2,1)S(1)} %shard_map.20), channel_id=1, source_target_pairs={{1,2},{2,1},{5,6},{6,5},{9,10},{10,9},{13,14},{14,13},{17,18},{18,... | collective-permute-start | bytes 811016 | tf_op jit(solution)/shard_map/ppermute | solution.py:390
  95.4 6.3 %shard_map.19.refs_0_.pre = f32[90,23,1024]{2,1,0:T(8,128)S(1)} custom-call(bf16[90,23,1024]{2,1,0:T(8,128)(2,1)S(1)} %bitcast.10, bf16[19,16,1024]{2,1,0:T(8,128)(2,1)S(1)} %collective-permute-done.edge_off.off, bf16[20,16,1024]{2,1,0:T(8,128)(2,1)S(1)} %collective-permute-done.1.edge_on.on, bf16[70,16,1024]{2,1,0:T(8,128)(2,1)S(1)} %collective-permute-done.2.mid_on), custom_call_target="tpu_custom_call" | custom-call | flops 9000000 | bytes 90000 | tf_op jit(solution)/shard_map/pallas_call | solution.py:372
  101.8 4.5 %shard_map.24 = (f32[90,23,1024]{2,1,0:T(8,128)}, f32[20,23,512]{2,1,0:T(8,128)S(1)}) custom-call(f32[90,23,1024]{2,1,0:T(8,128)S(1)} %shard_map.19.refs_0_.pre, bf16[66,16,512]{2,1,0:T(8,128)(2,1)S(1)} %collective-permute-done.15.refs_1_, bf16[66,16,1024]{2,1,0:T(8,128)(2,1)S(1)} %collective-permute-done.4.refs_2_.mid_diag), custom_call_target="tpu_custom_call" | custom-call | flops 5000000 | bytes 50000 | tf_op jit(solution)/shard_map/pallas_call | solution.py:462
  106.2 2.7 %shard_map.26 = (f32[90,23,1024]{2,1,0:T(8,128)}, f32[20,23,256]{2,1,0:T(8,128)S(1)}) custom-call(f32[90,23,1024]{2,1,0:T(8,128)S(1)} %shard_map.19.refs_0_.pre, bf16[66,16,256]{2,1,0:T(8,128)(2,1)S(1)} %collective-permute-done.16.mid_direct, bf16[66,16,1024]{2,1,0:T(8,128)(2,1)S(1)} %collective-permute-done.4.refs_2_.mid_diag, ...), custom_call_target="tpu_custom_call", output_to_operand_aliasing={{0}: (3, {})} | custom-call | flops 5000000 | bytes 50000 | tf_op jit(solution)/shard_map/pallas_call | solution.py:462
  109.0 2.7 %shard_map.27.rest_6_ = f32[90,23,1024]{2,1,0:T(8,128)} custom-call(f32[90,23,1024]{2,1,0:T(8,128)S(1)} %shard_map.19.refs_0_.pre, bf16[66,16,128]{2,1,0:T(8,128)(2,1)S(1)} %collective-permute-done.14.mid_direct, bf16[66,16,1024]{2,1,0:T(8,128)(2,1)S(1)} %collective-permute-done.4.refs_2_.mid_diag, ...), custom_call_target="tpu_custom_call", output_to_operand_aliasing={{}: (11, {})} | custom-call | flops 5000000 | bytes 50000 | tf_op jit(solution)/shard_map/pallas_call | solution.py:462
  111.7 2.2 %shard_map.28 = f32[90,23,1024]{2,1,0:T(8,128)} custom-call(f32[90,23,1024]{2,1,0:T(8,128)S(1)} %shard_map.19.refs_0_.pre, bf16[66,16,128]{2,1,0:T(8,128)(2,1)S(1)} %collective-permute-done.3.mid_direct, bf16[66,16,1024]{2,1,0:T(8,128)(2,1)S(1)} %collective-permute-done.4.refs_2_.mid_diag, ...), custom_call_target="tpu_custom_call", output_to_operand_aliasing={{}: (9, {})} | custom-call | flops 5000000 | bytes 50000 | tf_op jit(solution)/shard_map/pallas_call | solution.py:462
  (19 shorter events, 0.5 us)
Async XLA Ops:
  0.0 4.4 %copy-start = (bf16[23,90,1024]{2,0,1:T(8,128)(2,1)S(1)}, bf16[23,90,1024]{2,0,1:T(8,128)(2,1)}, u32[]{:S(2)}) copy-start(bf16[23,90,1024]{2,0,1:T(8,128)(2,1)} %param.1) | copy-start | bytes 12718084
  1.7 40.5 %collective-permute-start = (bf16[19,16,1024]{2,1,0:T(8,128)(2,1)S(1)}, bf16[19,16,1024]{2,1,0:T(8,128)(2,1)S(1)}, u32[]{:S(2)}, u32[]{:S(2)}) collective-permute-start(bf16[19,16,1024]{2,1,0:T(8,128)(2,1)S(1)} %get-tuple-element.15), channel_id=1, source_target_pairs={{1,2},{2,1},{3,4},{4,3},{5,6},{6,5},{7,8},{8,7},{9,10},{10,9},{11,... | collective-permute-start | bytes 1867784 | tf_op jit(solution)/shard_map/ppermute | solution.py:384
  4.5 86.5 %collective-permute-start.4 = (bf16[66,16,1024]{2,1,0:T(8,128)(2,1)S(1)}, bf16[66,16,1024]{2,1,0:T(8,128)(2,1)S(1)}, u32[]{:S(2)}, u32[]{:S(2)}) collective-permute-start(bf16[66,16,1024]{2,1,0:T(8,128)(2,1)S(1)} %shard_map.21), channel_id=1, source_target_pairs={{3,4},{4,3},{7,8},{8,7},{11,12},{12,11},{15,0},{0,15},{19,20},{20,... | collective-permute-start | bytes 6488072 | tf_op jit(solution)/shard_map/ppermute | solution.py:405
  5.2 40.7 %collective-permute-start.1 = (bf16[20,16,1024]{2,1,0:T(8,128)(2,1)S(1)}, bf16[20,16,1024]{2,1,0:T(8,128)(2,1)S(1)}, u32[]{:S(2)}, u32[]{:S(2)}) collective-permute-start(bf16[20,16,1024]{2,1,0:T(8,128)(2,1)S(1)} %get-tuple-element.16), channel_id=1, source_target_pairs={{0,1},{1,0},{2,3},{3,2},{4,5},{5,4},{6,7},{7,6},{8,9},{9,8},{10,11... | collective-permute-start | bytes 1966088 | tf_op jit(solution)/shard_map/ppermute | solution.py:385
  11.4 80.4 %collective-permute-start.2 = (bf16[70,16,1024]{2,1,0:T(8,128)(2,1)S(1)}, bf16[70,16,1024]{2,1,0:T(8,128)(2,1)S(1)}, u32[]{:S(2)}, u32[]{:S(2)}) collective-permute-start(bf16[70,16,1024]{2,1,0:T(8,128)(2,1)S(1)} %shard_map.18), channel_id=1, source_target_pairs={{0,1},{1,0},{2,3},{3,2},{4,5},{5,4},{6,7},{7,6},{8,9},{9,8},{10,11... | collective-permute-start | bytes 6881288 | tf_op jit(solution)/shard_map/ppermute | solution.py:404
  11.6 55.2 %collective-permute-start.15 = (bf16[66,16,512]{2,1,0:T(8,128)(2,1)S(1)}, bf16[66,16,512]{2,1,0:T(8,128)(2,1)S(1)}, u32[]{:S(2)}, u32[]{:S(2)}) collective-permute-start(bf16[66,16,512]{2,1,0:T(8,128)(2,1)S(1)} %shard_map.23), channel_id=1, source_target_pairs={{1,2},{2,1},{5,6},{6,5},{9,10},{10,9},{13,14},{14,13},{17,18},{18,... | collective-permute-start | bytes 3244040 | tf_op jit(solution)/shard_map/ppermute | solution.py:390
  42.2 14.8 %collective-permute-start.14 = (bf16[66,16,128]{2,1,0:T(8,128)(2,1)S(1)}, bf16[66,16,128]{2,1,0:T(8,128)(2,1)S(1)}, u32[]{:S(2)}, u32[]{:S(2)}) collective-permute-start(bf16[66,16,128]{2,1,0:T(8,128)(2,1)S(1)} %shard_map.22), channel_id=1, source_target_pairs={{1,2},{2,1},{5,6},{6,5},{9,10},{10,9},{13,14},{14,13},{17,18},{18,... | collective-permute-start | bytes 811016 | tf_op jit(solution)/shard_map/ppermute | solution.py:390
  46.0 20.1 %collective-permute-start.16 = (bf16[66,16,256]{2,1,0:T(8,128)(2,1)S(1)}, bf16[66,16,256]{2,1,0:T(8,128)(2,1)S(1)}, u32[]{:S(2)}, u32[]{:S(2)}) collective-permute-start(bf16[66,16,256]{2,1,0:T(8,128)(2,1)S(1)} %shard_map.25), channel_id=1, source_target_pairs={{1,2},{2,1},{5,6},{6,5},{9,10},{10,9},{13,14},{14,13},{17,18},{18,... | collective-permute-start | bytes 1622024 | tf_op jit(solution)/shard_map/ppermute | solution.py:390
  57.0 14.8 %collective-permute-start.10 = (f32[10,23,512]{2,1,0:T(8,128)S(1)}, f32[10,23,512]{2,1,0:T(8,128)S(1)}, u32[]{:S(2)}, u32[]{:S(2)}) collective-permute-start(f32[10,23,512]{2,1,0:T(8,128)S(1)} %get-tuple-element.20), channel_id=1, source_target_pairs={{113,18},{1,98},{114,17},{2,97},{117,22},{5,102},{118,21},{6,101},... | collective-permute-start | bytes 1413128 | tf_op jit(solution)/shard_map/ppermute | solution.py:429
  66.1 8.1 %collective-permute-start.12 = (f32[10,23,512]{2,1,0:T(8,128)S(1)}, f32[10,23,512]{2,1,0:T(8,128)S(1)}, u32[]{:S(2)}, u32[]{:S(2)}) collective-permute-start(f32[10,23,512]{2,1,0:T(8,128)S(1)} %get-tuple-element.20), channel_id=1, source_target_pairs={{112,51},{0,67},{115,48},{3,64},{116,55},{4,71},{119,52},{7,68},{1... | collective-permute-start | bytes 1413128 | tf_op jit(solution)/shard_map/ppermute | solution.py:429
  66.8 8.7 %collective-permute-start.8 = (f32[10,23,512]{2,1,0:T(8,128)S(1)}, f32[10,23,512]{2,1,0:T(8,128)S(1)}, u32[]{:S(2)}, u32[]{:S(2)}) collective-permute-start(f32[10,23,512]{2,1,0:T(8,128)S(1)} %get-tuple-element.19), channel_id=1, source_target_pairs={{112,35},{0,83},{115,32},{3,80},{116,39},{4,87},{119,36},{7,84},{1... | collective-permute-start | bytes 1413128 | tf_op jit(solution)/shard_map/ppermute | solution.py:429
  71.8 16.1 %collective-permute-start.7 = (f32[10,23,512]{2,1,0:T(8,128)S(1)}, f32[10,23,512]{2,1,0:T(8,128)S(1)}, u32[]{:S(2)}, u32[]{:S(2)}) collective-permute-start(f32[10,23,512]{2,1,0:T(8,128)S(1)} %get-tuple-element.19), channel_id=1, source_target_pairs={{113,129},{1,241},{114,130},{2,242},{117,133},{5,245},{118,134},{6... | collective-permute-start | bytes 1413128 | tf_op jit(solution)/shard_map/ppermute | solution.py:431
  74.2 16.1 %collective-permute-start.11 = (f32[10,23,512]{2,1,0:T(8,128)S(1)}, f32[10,23,512]{2,1,0:T(8,128)S(1)}, u32[]{:S(2)}, u32[]{:S(2)}) collective-permute-start(f32[10,23,512]{2,1,0:T(8,128)S(1)} %collective-permute-done.10), channel_id=1, source_target_pairs={{18,129},{98,241},{17,130},{97,242},{22,133},{102,245},{21,134},{1... | collective-permute-start | bytes 1413128 | tf_op jit(solution)/shard_map/ppermute | solution.py:430
  75.5 33.5 %collective-permute-start.5 = (f32[10,23,1024]{2,1,0:T(8,128)S(1)}, f32[10,23,1024]{2,1,0:T(8,128)S(1)}, u32[]{:S(2)}, u32[]{:S(2)}) collective-permute-start(f32[10,23,1024]{2,1,0:T(8,128)S(1)} %get-tuple-element.17), channel_id=1, source_target_pairs={{0,16},{16,32},{32,48},{48,64},{64,80},{80,96},{96,112},{128,144},... | collective-permute-start | bytes 2826248 | tf_op jit(solution)/shard_map/ppermute | solution.py:433
  87.9 21.1 %collective-permute-start.6 = (f32[10,23,1024]{2,1,0:T(8,128)S(1)}, f32[10,23,1024]{2,1,0:T(8,128)S(1)}, u32[]{:S(2)}, u32[]{:S(2)}) collective-permute-start(f32[10,23,1024]{2,1,0:T(8,128)S(1)} %get-tuple-element.18), channel_id=1, source_target_pairs={{16,0},{32,16},{48,32},{64,48},{80,64},{96,80},{112,96},{144,128},... | collective-permute-start | bytes 2826248 | tf_op jit(solution)/shard_map/ppermute | solution.py:434
  90.3 18.7 %collective-permute-start.13 = (f32[10,23,512]{2,1,0:T(8,128)S(1)}, f32[10,23,512]{2,1,0:T(8,128)S(1)}, u32[]{:S(2)}, u32[]{:S(2)}) collective-permute-start(f32[10,23,512]{2,1,0:T(8,128)S(1)} %collective-permute-done.12), channel_id=1, source_target_pairs={{51,128},{67,240},{48,131},{64,243},{55,132},{71,244},{52,135},{68... | collective-permute-start | bytes 1413128 | tf_op jit(solution)/shard_map/ppermute | solution.py:430
  91.0 18.0 %collective-permute-start.9 = (f32[10,23,512]{2,1,0:T(8,128)S(1)}, f32[10,23,512]{2,1,0:T(8,128)S(1)}, u32[]{:S(2)}, u32[]{:S(2)}) collective-permute-start(f32[10,23,512]{2,1,0:T(8,128)S(1)} %collective-permute-done.8), channel_id=1, source_target_pairs={{35,128},{83,240},{32,131},{80,243},{39,132},{87,244},{36,135},{84... | collective-permute-start | bytes 1413128 | tf_op jit(solution)/shard_map/ppermute | solution.py:430
  91.8 19.9 %collective-permute-start.3 = (bf16[66,16,128]{2,1,0:T(8,128)(2,1)S(1)}, bf16[66,16,128]{2,1,0:T(8,128)(2,1)S(1)}, u32[]{:S(2)}, u32[]{:S(2)}) collective-permute-start(bf16[66,16,128]{2,1,0:T(8,128)(2,1)S(1)} %shard_map.20), channel_id=1, source_target_pairs={{1,2},{2,1},{5,6},{6,5},{9,10},{10,9},{13,14},{14,13},{17,18},{18,... | collective-permute-start | bytes 811016 | tf_op jit(solution)/shard_map/ppermute | solution.py:390

commit v4 on v3

--- a/solution.py
+++ b/solution.py
@@ -15,7 +15,7 @@
 SCALE = 1.0 / (DAY_WIN * LON_WIN)
 BLOCK = 256
 WIDTHS = (512, 256, 128, 128)
-AHEAD = 2
+JOINS = {2: (0,), 3: (1, 2)}
 VMEM = pl.BlockSpec(memory_space=pltpu.VMEM)
 ANY = pl.BlockSpec(memory_space=pl.ANY)
 
@@ -221,15 +221,14 @@
     return jnp.where(direct, a[j, :, cols], b[j, :, cols])
 
 
-def main_kernel(planes, start, joined, pre, mid_direct, mid_diag, *rest):
-    lon_args, moving = None, []
-    if joined:
-        lon_args, done, (prev, out, g, buf, sems, *spare) = rest[:6], rest[6 : 6 + len(joined)], rest[6 + len(joined) :]
-        moving = start_join(planes, joined, lon_args, done, out, *spare)
-    elif planes:
-        *lon_args, prev, out, g, buf, sems = rest
+def main_kernel(planes, start, own_join, joined, lon_count, pre, mid_direct, mid_diag, *rest):
+    lon_args, rest = rest[:lon_count], rest[lon_count:]
+    done, rest = rest[: len(joined)], rest[len(joined) :]
+    if own_join:
+        prev, out, g, buf, sems, *spare = rest
     else:
-        prev, out, ends, g, buf, sems = rest
+        prev, out, ends, g, buf, sems, *spare = rest
+    moving = start_join(planes, joined, lon_args, done, out, *spare) if joined else []
     lons, days, _ = pre.shape
     width = mid_direct.shape[2]
     high = lons - LON_HALF
@@ -242,7 +241,7 @@
     base = (lons - buf.shape[1]) // 2
     parts = sems.shape[1]
     step = buf.shape[1] // parts
-    if planes:
+    if own_join:
         z = lax.axis_index("lon") % planes
         gains = jnp.where(z == 0, 1.0, 0.0), jnp.where(z == planes - 1, 1.0, 0.0)
 
@@ -268,7 +267,7 @@
             g[LON_HALF + i] = pre[LON_HALF + i, :, cols] + dot(tile_mat, off)
             return 0
 
-        lax.fori_loop(0, tiles, inner, 0, unroll=11)
+        lax.fori_loop(0, tiles, inner, 0, unroll=True)
         for q in range(mid - tiles):
             at = slice(q * DAY_HALF, (q + 1) * DAY_HALF)
             off = jnp.where(direct, mid_direct[at, :, local_cols], mid_diag[at, :, cols])
@@ -281,7 +280,7 @@
         moves = list(copies(b))
 
         def end(side, j, total):
-            if not planes:
+            if not own_join:
                 ends[side * LON_HALF + j, :, local_cols] = total
                 return
             near = lon_args[side][j, :, cols]
@@ -305,14 +304,14 @@
         at = LON_HALF + 1
         for k in range(parts):
             to = min(base + (k + 1) * step, high)
-            total = lax.fori_loop(at, to, center, total, unroll=5)
+            total = lax.fori_loop(at, to, center, total, unroll=True)
             at = to
-            if k < parts - 1 or not planes:
+            if k < parts - 1 or not own_join:
                 moves[k].start()
         for j in range(LON_HALF):
             total = total - g[high + j - LON_HALF - 1]
             end(1, j, total)
-        if planes:
+        if own_join:
             moves[-1].start()
     for b in range(max(0, blocks - 2), blocks):
         for copy in copies(b):
@@ -323,7 +322,7 @@
 
 def start_join(planes, starts, lon_args, ends, out, buf, sems):
     from_l, from_r, *far_args = lon_args
-    width = buf.shape[3]
+    base, width = starts[0], buf.shape[3]
     high = out.shape[0] - LON_HALF
     day, z = lax.axis_index("day"), lax.axis_index("lon") % planes
     direct = is_direct(day)
@@ -339,11 +338,11 @@
                 def add(j, _):
                     far = far_value(direct, far_args, j, at, block)
                     value = end[side * LON_HALF + j, :, own_cols] + near[j, :, cols] + far * gain
-                    buf[side, j, :, cols] = value * SCALE
+                    buf[side, j, :, slice(at - base, at - base + block)] = value * SCALE
                     return 0
 
                 lax.fori_loop(0, LON_HALF, add, 0, unroll=5)
-        moves.append(pltpu.make_async_copy(buf.at[side], out.at[row : row + LON_HALF, :, :width], sems.at[side]))
+        moves.append(pltpu.make_async_copy(buf.at[side], out.at[row : row + LON_HALF, :, base : base + width], sems.at[side]))
         moves[-1].start()
     return moves
 
@@ -438,12 +437,13 @@
     whole = jax.ShapeDtypeStruct(field.shape, jnp.float32)
     out, ends = None, []
     for c, width in enumerate(WIDTHS):
-        own_join = c >= AHEAD
-        joined = starts[:AHEAD] if c == AHEAD else []
+        joined = JOINS.get(c, ())
+        own_join = c == len(WIDTHS) - 1
+        needs = lon_args if own_join else lon_args[:4] if joined else []
         block = min(BLOCK, width)
-        args = [pre, mid_direct[c], mid_diag] + (lon_args if own_join else []) + (ends if joined else [])
+        args = [pre, mid_direct[c], mid_diag, *needs, *(ends[k] for k in joined)]
         specs = [VMEM] * len(args)
-        body = functools.partial(main_kernel, nz if own_join else 0, starts[c], joined)
+        body = functools.partial(main_kernel, nz, starts[c], own_join, [starts[k] for k in joined], len(needs))
         if c:
             specs.append(ANY)
             args.append(out)
@@ -457,7 +457,7 @@
             pltpu.SemaphoreType.DMA((slots, 3 if own_join else 2)),
         ]
         if joined:
-            scratch += [pltpu.VMEM((2, LON_HALF, days, starts[c]), jnp.float32), pltpu.SemaphoreType.DMA((2,))]
+            scratch += [pltpu.VMEM((2, LON_HALF, days, sum(WIDTHS[k] for k in joined)), jnp.float32), pltpu.SemaphoreType.DMA((2,))]
         tail = jax.ShapeDtypeStruct((2 * LON_HALF, days, width), jnp.float32)
         res = pl.pallas_call(
             fn,

time: 114 us -> 110 us (0.965)
  Pallas kernels: 20.3 us -> 15.6 us
  waiting for transfers between devices: 48.9 us -> 52.3 us
  starting transfers between devices: 42.9 us -> 39.8 us
    ppermute x1, starting transfers between devices: 2.36 us -> 10.3 us  [local(): landed.insert(0, lax.ppermute(first, both_axes, straight))]
    ppermute x3, starting transfers between devices: 10.5 us -> 2.69 us  [local(): hopped = lax.ppermute(x, both_axes, hop)]
    ppermute x4, waiting for transfers between devices: 8.11 us -> 12.9 us  [local(): mid_direct.append(lax.ppermute(off, 'day', swap(1, 4)))]
    pallas_call x4, Pallas kernels: 12.1 us -> 7.39 us  [local(): pl.pallas_call(fn, in_specs=specs, out_specs=[ANY] if own_join else [ANY,...]
    ppermute x1, starting transfers between devices: 5.53 us -> 1.34 us  [local(): from_l = lax.ppermute(to_right, 'lon', [(i, i + 1) for i in inner])]
    ppermute x3, waiting for transfers between devices: 4.31 us -> 0.49 us  [local(): hopped = lax.ppermute(x, both_axes, hop)]
    ppermute x3, waiting for transfers between devices: 1.05 us -> 3.19 us  [local(): landed.append(lax.ppermute(hopped, both_axes, land))]
  transfers between devices with their start and end apart: 17 -> 17, of which waited for: 5 -> 6; matrix products, arithmetic and copies ran while one was open for 0% -> 0% of each run, Pallas kernels for 16% -> 12%
where the time goes in v4:
time: 110 us; the launch traced here: 109 us
  waiting for transfers between devices  52.3 us (48%)
  starting transfers between devices  39.8 us (36%)
  Pallas kernels  15.6 us (14%)
  local copies, waits for them, and re-layouts  1.4 us (1%)
    ppermute x1, waiting for transfers between devices, local(): edge_off = lax.ppermute(e_off, 'day', swap(1, 2))  28.5 us
    ppermute x4, waiting for transfers between devices, local(): mid_direct.append(lax.ppermute(off, 'day', swap(1, 4)))  12.9 us
    ppermute x4, starting transfers between devices, local(): mid_direct.append(lax.ppermute(off, 'day', swap(1, 4)))  12 us
    ppermute x1, starting transfers between devices, local(): landed.insert(0, lax.ppermute(first, both_axes, straight))  10.3 us
    pallas_call x4, Pallas kernels, local(): pl.pallas_call(fn, in_specs=specs, out_specs=[ANY] if own_join else [ANY,...  7.39 us
    pallas_call x8, Pallas kernels, call(): pl.pallas_call(body, in_specs=[VMEM] * len(args), out_specs=[VMEM] * len(...  7.25 us
    ppermute x1, waiting for transfers between devices, local(): landed.insert(0, lax.ppermute(first, both_axes, straight))  7.14 us
    ppermute x1, starting transfers between devices, local(): edge_on = lax.ppermute(e_on, 'day', swap(0, 2))  5.86 us
  transfers between devices with their start and end apart: 17, of which 6 were waited for; matrix products, arithmetic and copies ran while one was open for 0% of the time, Pallas kernels for 12%

profile of v4, /device:TPU:1, one launch (start us, length us, event | category | flops | bytes accessed | tf_op | source)
XLA Modules:
  0.0 109.4 jit_solution(6707068955682939093)
XLA Ops:
  0.0 1.4 %fusion = (bf16[10,23,1024]{2,1,0:T(8,128)(2,1)S(1)}, bf16[10,23,1024]{2,1,0:T(8,128)(2,1)S(1)}) fusion(bf16[90,23,1024]{2,1,0:T(8,128)(2,1)} %bitcast.2), kind=kLoop, calls=%fused_computation.1 | loop fusion | bytes 1884160 | tf_op jit(solution)/shard_map/slice | solution.py:380
  1.5 0.2 shard_map.17
  1.7 2.8 %collective-permute-start = (bf16[19,16,1024]{2,1,0:T(8,128)(2,1)S(1)}, bf16[19,16,1024]{2,1,0:T(8,128)(2,1)S(1)}, u32[]{:S(2)}, u32[]{:S(2)}) collective-permute-start(bf16[19,16,1024]{2,1,0:T(8,128)(2,1)S(1)} %get-tuple-element.17), channel_id=1, source_target_pairs={{1,2},{2,1},{3,4},{4,3},{5,6},{6,5},{7,8},{8,7},{9,10},{10,9},{11,... | collective-permute-start | bytes 1867784 | tf_op jit(solution)/shard_map/ppermute | solution.py:383
  4.5 0.8 collective-permute-start.4
  5.2 5.9 %collective-permute-start.1 = (bf16[20,16,1024]{2,1,0:T(8,128)(2,1)S(1)}, bf16[20,16,1024]{2,1,0:T(8,128)(2,1)S(1)}, u32[]{:S(2)}, u32[]{:S(2)}) collective-permute-start(bf16[20,16,1024]{2,1,0:T(8,128)(2,1)S(1)} %get-tuple-element.18), channel_id=1, source_target_pairs={{0,1},{1,0},{2,3},{3,2},{4,5},{5,4},{6,7},{7,6},{8,9},{9,8},{10,11... | collective-permute-start | bytes 1966088 | tf_op jit(solution)/shard_map/ppermute | solution.py:384
  11.1 0.3 shard_map.18
  11.5 0.1 shard_map.23
  11.6 1.9 %collective-permute-start.15 = (bf16[66,16,512]{2,1,0:T(8,128)(2,1)S(1)}, bf16[66,16,512]{2,1,0:T(8,128)(2,1)S(1)}, u32[]{:S(2)}, u32[]{:S(2)}) collective-permute-start(bf16[66,16,512]{2,1,0:T(8,128)(2,1)S(1)} %shard_map.23), channel_id=1, source_target_pairs={{1,2},{2,1},{5,6},{6,5},{9,10},{10,9},{13,14},{14,13},{17,18},{18,... | collective-permute-start | bytes 3244040 | tf_op jit(solution)/shard_map/ppermute | solution.py:389
  13.7 28.5 %collective-permute-done.edge_off.off = bf16[19,16,1024]{2,1,0:T(8,128)(2,1)S(1)} collective-permute-done((bf16[19,16,1024]{2,1,0:T(8,128)(2,1)S(1)}, bf16[19,16,1024]{2,1,0:T(8,128)(2,1)S(1)}, u32[]{:S(2)}, u32[]{:S(2)}) %collective-permute-start) | collective-permute-done | bytes 622624 | tf_op jit(solution)/shard_map/ppermute | solution.py:383
  42.2 3.6 %collective-permute-start.16 = (bf16[66,16,128]{2,1,0:T(8,128)(2,1)S(1)}, bf16[66,16,128]{2,1,0:T(8,128)(2,1)S(1)}, u32[]{:S(2)}, u32[]{:S(2)}) collective-permute-start(bf16[66,16,128]{2,1,0:T(8,128)(2,1)S(1)} %shard_map.26), channel_id=1, source_target_pairs={{1,2},{2,1},{5,6},{6,5},{9,10},{10,9},{13,14},{14,13},{17,18},{18,... | collective-permute-start | bytes 811016 | tf_op jit(solution)/shard_map/ppermute | solution.py:389
  46.0 1.9 %collective-permute-start.14 = (bf16[66,16,256]{2,1,0:T(8,128)(2,1)S(1)}, bf16[66,16,256]{2,1,0:T(8,128)(2,1)S(1)}, u32[]{:S(2)}, u32[]{:S(2)}) collective-permute-start(bf16[66,16,256]{2,1,0:T(8,128)(2,1)S(1)} %shard_map.22), channel_id=1, source_target_pairs={{1,2},{2,1},{5,6},{6,5},{9,10},{10,9},{13,14},{14,13},{17,18},{18,... | collective-permute-start | bytes 1622024 | tf_op jit(solution)/shard_map/ppermute | solution.py:389
  47.9 1.0 edge.1
  48.9 8.1 %collective-permute-done.16.mid_direct = bf16[66,16,128]{2,1,0:T(8,128)(2,1)S(1)} collective-permute-done((bf16[66,16,128]{2,1,0:T(8,128)(2,1)S(1)}, bf16[66,16,128]{2,1,0:T(8,128)(2,1)S(1)}, u32[]{:S(2)}, u32[]{:S(2)}) %collective-permute-start.16) | collective-permute-done | bytes 270368 | tf_op jit(solution)/shard_map/ppermute | solution.py:389
  57.0 0.7 collective-permute-start.8
  57.7 4.8 %collective-permute-done.14.mid_direct = bf16[66,16,256]{2,1,0:T(8,128)(2,1)S(1)} collective-permute-done((bf16[66,16,256]{2,1,0:T(8,128)(2,1)S(1)}, bf16[66,16,256]{2,1,0:T(8,128)(2,1)S(1)}, u32[]{:S(2)}, u32[]{:S(2)}) %collective-permute-start.14) | collective-permute-done | bytes 540704 | tf_op jit(solution)/shard_map/ppermute | solution.py:389
  62.5 10.3 %collective-permute-start.7 = (f32[10,23,512]{2,1,0:T(8,128)S(1)}, f32[10,23,512]{2,1,0:T(8,128)S(1)}, u32[]{:S(2)}, u32[]{:S(2)}) collective-permute-start(f32[10,23,512]{2,1,0:T(8,128)S(1)} %get-tuple-element.21), channel_id=1, source_target_pairs={{113,129},{1,241},{114,130},{2,242},{117,133},{5,245},{118,134},{6... | collective-permute-start | bytes 1413128 | tf_op jit(solution)/shard_map/ppermute | solution.py:430
  72.8 1.3 %collective-permute-start.10 = (f32[10,23,512]{2,1,0:T(8,128)S(1)}, f32[10,23,512]{2,1,0:T(8,128)S(1)}, u32[]{:S(2)}, u32[]{:S(2)}) collective-permute-start(f32[10,23,512]{2,1,0:T(8,128)S(1)} %get-tuple-element.22), channel_id=1, source_target_pairs={{113,18},{1,98},{114,17},{2,97},{117,22},{5,102},{118,21},{6,101},... | collective-permute-start | bytes 1413128 | tf_op jit(solution)/shard_map/ppermute | solution.py:428
  74.1 0.7 collective-permute-start.12
  74.8 7.1 %collective-permute-done.7.rest_2_ = f32[10,23,512]{2,1,0:T(8,128)S(1)} collective-permute-done((f32[10,23,512]{2,1,0:T(8,128)S(1)}, f32[10,23,512]{2,1,0:T(8,128)S(1)}, u32[]{:S(2)}, u32[]{:S(2)}) %collective-permute-start.7) | collective-permute-done | bytes 471072 | tf_op jit(solution)/shard_map/ppermute | solution.py:430
  82.0 1.3 %collective-permute-start.5 = (f32[10,23,1024]{2,1,0:T(8,128)S(1)}, f32[10,23,1024]{2,1,0:T(8,128)S(1)}, u32[]{:S(2)}, u32[]{:S(2)}) collective-permute-start(f32[10,23,1024]{2,1,0:T(8,128)S(1)} %get-tuple-element.19), channel_id=1, source_target_pairs={{0,16},{16,32},{32,48},{48,64},{64,80},{80,96},{96,112},{128,144},... | collective-permute-start | bytes 2826248 | tf_op jit(solution)/shard_map/ppermute | solution.py:432
  83.3 0.5 collective-permute-done.10
  83.8 1.3 %collective-permute-start.6 = (f32[10,23,1024]{2,1,0:T(8,128)S(1)}, f32[10,23,1024]{2,1,0:T(8,128)S(1)}, u32[]{:S(2)}, u32[]{:S(2)}) collective-permute-start(f32[10,23,1024]{2,1,0:T(8,128)S(1)} %get-tuple-element.20), channel_id=1, source_target_pairs={{16,0},{32,16},{48,32},{64,48},{80,64},{96,80},{112,96},{144,128},... | collective-permute-start | bytes 2826248 | tf_op jit(solution)/shard_map/ppermute | solution.py:433
  85.1 0.7 collective-permute-start.9
  85.8 1.3 %collective-permute-start.11 = (f32[10,23,512]{2,1,0:T(8,128)S(1)}, f32[10,23,512]{2,1,0:T(8,128)S(1)}, u32[]{:S(2)}, u32[]{:S(2)}) collective-permute-start(f32[10,23,512]{2,1,0:T(8,128)S(1)} %collective-permute-done.10), channel_id=1, source_target_pairs={{18,129},{98,241},{17,130},{97,242},{22,133},{102,245},{21,134},{1... | collective-permute-start | bytes 1413128 | tf_op jit(solution)/shard_map/ppermute | solution.py:429
  87.1 0.7 collective-permute-start.13
  88.0 4.5 %collective-permute-start.3 = (bf16[66,16,128]{2,1,0:T(8,128)(2,1)S(1)}, bf16[66,16,128]{2,1,0:T(8,128)(2,1)S(1)}, u32[]{:S(2)}, u32[]{:S(2)}) collective-permute-start(bf16[66,16,128]{2,1,0:T(8,128)(2,1)S(1)} %shard_map.20), channel_id=1, source_target_pairs={{1,2},{2,1},{5,6},{6,5},{9,10},{10,9},{13,14},{14,13},{17,18},{18,... | collective-permute-start | bytes 811016 | tf_op jit(solution)/shard_map/ppermute | solution.py:389
  92.5 6.3 %shard_map.19.refs_0_.pre = f32[90,23,1024]{2,1,0:T(8,128)S(1)} custom-call(bf16[90,23,1024]{2,1,0:T(8,128)(2,1)S(1)} %bitcast.10, bf16[19,16,1024]{2,1,0:T(8,128)(2,1)S(1)} %collective-permute-done.edge_off.off, bf16[20,16,1024]{2,1,0:T(8,128)(2,1)S(1)} %collective-permute-done.1.edge_on.on, bf16[70,16,1024]{2,1,0:T(8,128)(2,1)S(1)} %collective-permute-done.2.mid_on), custom_call_target="tpu_custom_call" | custom-call | flops 9000000 | bytes 90000 | tf_op jit(solution)/shard_map/pallas_call | solution.py:371
  98.8 2.3 %shard_map.24 = (f32[90,23,1024]{2,1,0:T(8,128)}, f32[20,23,512]{2,1,0:T(8,128)S(1)}) custom-call(f32[90,23,1024]{2,1,0:T(8,128)S(1)} %shard_map.19.refs_0_.pre, bf16[66,16,512]{2,1,0:T(8,128)(2,1)S(1)} %collective-permute-done.15.refs_1_, bf16[66,16,1024]{2,1,0:T(8,128)(2,1)S(1)} %collective-permute-done.4.refs_2_.mid_diag), custom_call_target="tpu_custom_call" | custom-call | flops 5000000 | bytes 50000 | tf_op jit(solution)/shard_map/pallas_call | solution.py:462
  101.1 1.7 %shard_map.25 = (f32[90,23,1024]{2,1,0:T(8,128)}, f32[20,23,256]{2,1,0:T(8,128)S(1)}) custom-call(f32[90,23,1024]{2,1,0:T(8,128)S(1)} %shard_map.19.refs_0_.pre, bf16[66,16,256]{2,1,0:T(8,128)(2,1)S(1)} %collective-permute-done.14.mid_direct, bf16[66,16,1024]{2,1,0:T(8,128)(2,1)S(1)} %collective-permute-done.4.refs_2_.mid_diag, ...), custom_call_target="tpu_custom_call", output_to_operand_aliasing={{0}: (3, {})} | custom-call | flops 5000000 | bytes 50000 | tf_op jit(solution)/shard_map/pallas_call | solution.py:462
  102.8 1.7 %shard_map.27 = (f32[90,23,1024]{2,1,0:T(8,128)}, f32[20,23,128]{2,1,0:T(8,128)S(1)}) custom-call(f32[90,23,1024]{2,1,0:T(8,128)S(1)} %shard_map.19.refs_0_.pre, bf16[66,16,128]{2,1,0:T(8,128)(2,1)S(1)} %collective-permute-done.16.mid_direct, bf16[66,16,1024]{2,1,0:T(8,128)(2,1)S(1)} %collective-permute-done.4.refs_2_.mid_diag, ...), custom_call_target="tpu_custom_call", output_to_operand_aliasing={{0}: (8, {})} | custom-call | flops 5000000 | bytes 50000 | tf_op jit(solution)/shard_map/pallas_call | solution.py:462
  104.5 3.2 %collective-permute-done.11.rest_4_ = f32[10,23,512]{2,1,0:T(8,128)S(1)} collective-permute-done((f32[10,23,512]{2,1,0:T(8,128)S(1)}, f32[10,23,512]{2,1,0:T(8,128)S(1)}, u32[]{:S(2)}, u32[]{:S(2)}) %collective-permute-start.11) | collective-permute-done | bytes 471072 | tf_op jit(solution)/shard_map/ppermute | solution.py:429
  107.7 1.8 %shard_map.28 = f32[90,23,1024]{2,1,0:T(8,128)} custom-call(f32[90,23,1024]{2,1,0:T(8,128)S(1)} %shard_map.19.refs_0_.pre, bf16[66,16,128]{2,1,0:T(8,128)(2,1)S(1)} %collective-permute-done.3.mid_direct, bf16[66,16,1024]{2,1,0:T(8,128)(2,1)S(1)} %collective-permute-done.4.refs_2_.mid_diag, ...), custom_call_target="tpu_custom_call", output_to_operand_aliasing={{}: (11, {})} | custom-call | flops 5000000 | bytes 50000 | tf_op jit(solution)/shard_map/pallas_call | solution.py:462
  (19 shorter events, 0.6 us)
Async XLA Ops:
  0.0 4.4 %copy-start = (bf16[23,90,1024]{2,0,1:T(8,128)(2,1)S(1)}, bf16[23,90,1024]{2,0,1:T(8,128)(2,1)}, u32[]{:S(2)}) copy-start(bf16[23,90,1024]{2,0,1:T(8,128)(2,1)} %param.1) | copy-start | bytes 12718084
  1.7 40.5 %collective-permute-start = (bf16[19,16,1024]{2,1,0:T(8,128)(2,1)S(1)}, bf16[19,16,1024]{2,1,0:T(8,128)(2,1)S(1)}, u32[]{:S(2)}, u32[]{:S(2)}) collective-permute-start(bf16[19,16,1024]{2,1,0:T(8,128)(2,1)S(1)} %get-tuple-element.17), channel_id=1, source_target_pairs={{1,2},{2,1},{3,4},{4,3},{5,6},{6,5},{7,8},{8,7},{9,10},{10,9},{11,... | collective-permute-start | bytes 1867784 | tf_op jit(solution)/shard_map/ppermute | solution.py:383
  4.5 82.7 %collective-permute-start.4 = (bf16[66,16,1024]{2,1,0:T(8,128)(2,1)S(1)}, bf16[66,16,1024]{2,1,0:T(8,128)(2,1)S(1)}, u32[]{:S(2)}, u32[]{:S(2)}) collective-permute-start(bf16[66,16,1024]{2,1,0:T(8,128)(2,1)S(1)} %shard_map.21), channel_id=1, source_target_pairs={{3,4},{4,3},{7,8},{8,7},{11,12},{12,11},{15,0},{0,15},{19,20},{20,... | collective-permute-start | bytes 6488072 | tf_op jit(solution)/shard_map/ppermute | solution.py:404
  5.2 40.7 %collective-permute-start.1 = (bf16[20,16,1024]{2,1,0:T(8,128)(2,1)S(1)}, bf16[20,16,1024]{2,1,0:T(8,128)(2,1)S(1)}, u32[]{:S(2)}, u32[]{:S(2)}) collective-permute-start(bf16[20,16,1024]{2,1,0:T(8,128)(2,1)S(1)} %get-tuple-element.18), channel_id=1, source_target_pairs={{0,1},{1,0},{2,3},{3,2},{4,5},{5,4},{6,7},{7,6},{8,9},{9,8},{10,11... | collective-permute-start | bytes 1966088 | tf_op jit(solution)/shard_map/ppermute | solution.py:384
  11.4 76.6 %collective-permute-start.2 = (bf16[70,16,1024]{2,1,0:T(8,128)(2,1)S(1)}, bf16[70,16,1024]{2,1,0:T(8,128)(2,1)S(1)}, u32[]{:S(2)}, u32[]{:S(2)}) collective-permute-start(bf16[70,16,1024]{2,1,0:T(8,128)(2,1)S(1)} %shard_map.18), channel_id=1, source_target_pairs={{0,1},{1,0},{2,3},{3,2},{4,5},{5,4},{6,7},{7,6},{8,9},{9,8},{10,11... | collective-permute-start | bytes 6881288 | tf_op jit(solution)/shard_map/ppermute | solution.py:403
  11.6 61.1 %collective-permute-start.15 = (bf16[66,16,512]{2,1,0:T(8,128)(2,1)S(1)}, bf16[66,16,512]{2,1,0:T(8,128)(2,1)S(1)}, u32[]{:S(2)}, u32[]{:S(2)}) collective-permute-start(bf16[66,16,512]{2,1,0:T(8,128)(2,1)S(1)} %shard_map.23), channel_id=1, source_target_pairs={{1,2},{2,1},{5,6},{6,5},{9,10},{10,9},{13,14},{14,13},{17,18},{18,... | collective-permute-start | bytes 3244040 | tf_op jit(solution)/shard_map/ppermute | solution.py:389
  42.2 14.8 %collective-permute-start.16 = (bf16[66,16,128]{2,1,0:T(8,128)(2,1)S(1)}, bf16[66,16,128]{2,1,0:T(8,128)(2,1)S(1)}, u32[]{:S(2)}, u32[]{:S(2)}) collective-permute-start(bf16[66,16,128]{2,1,0:T(8,128)(2,1)S(1)} %shard_map.26), channel_id=1, source_target_pairs={{1,2},{2,1},{5,6},{6,5},{9,10},{10,9},{13,14},{14,13},{17,18},{18,... | collective-permute-start | bytes 811016 | tf_op jit(solution)/shard_map/ppermute | solution.py:389
  46.0 16.5 %collective-permute-start.14 = (bf16[66,16,256]{2,1,0:T(8,128)(2,1)S(1)}, bf16[66,16,256]{2,1,0:T(8,128)(2,1)S(1)}, u32[]{:S(2)}, u32[]{:S(2)}) collective-permute-start(bf16[66,16,256]{2,1,0:T(8,128)(2,1)S(1)} %shard_map.22), channel_id=1, source_target_pairs={{1,2},{2,1},{5,6},{6,5},{9,10},{10,9},{13,14},{14,13},{17,18},{18,... | collective-permute-start | bytes 1622024 | tf_op jit(solution)/shard_map/ppermute | solution.py:389
  57.0 17.1 %collective-permute-start.8 = (f32[10,23,512]{2,1,0:T(8,128)S(1)}, f32[10,23,512]{2,1,0:T(8,128)S(1)}, u32[]{:S(2)}, u32[]{:S(2)}) collective-permute-start(f32[10,23,512]{2,1,0:T(8,128)S(1)} %get-tuple-element.21), channel_id=1, source_target_pairs={{112,35},{0,83},{115,32},{3,80},{116,39},{4,87},{119,36},{7,84},{1... | collective-permute-start | bytes 1413128 | tf_op jit(solution)/shard_map/ppermute | solution.py:428
  62.5 19.5 %collective-permute-start.7 = (f32[10,23,512]{2,1,0:T(8,128)S(1)}, f32[10,23,512]{2,1,0:T(8,128)S(1)}, u32[]{:S(2)}, u32[]{:S(2)}) collective-permute-start(f32[10,23,512]{2,1,0:T(8,128)S(1)} %get-tuple-element.21), channel_id=1, source_target_pairs={{113,129},{1,241},{114,130},{2,242},{117,133},{5,245},{118,134},{6... | collective-permute-start | bytes 1413128 | tf_op jit(solution)/shard_map/ppermute | solution.py:430
  72.8 11.0 %collective-permute-start.10 = (f32[10,23,512]{2,1,0:T(8,128)S(1)}, f32[10,23,512]{2,1,0:T(8,128)S(1)}, u32[]{:S(2)}, u32[]{:S(2)}) collective-permute-start(f32[10,23,512]{2,1,0:T(8,128)S(1)} %get-tuple-element.22), channel_id=1, source_target_pairs={{113,18},{1,98},{114,17},{2,97},{117,22},{5,102},{118,21},{6,101},... | collective-permute-start | bytes 1413128 | tf_op jit(solution)/shard_map/ppermute | solution.py:428
  74.1 11.0 %collective-permute-start.12 = (f32[10,23,512]{2,1,0:T(8,128)S(1)}, f32[10,23,512]{2,1,0:T(8,128)S(1)}, u32[]{:S(2)}, u32[]{:S(2)}) collective-permute-start(f32[10,23,512]{2,1,0:T(8,128)S(1)} %get-tuple-element.22), channel_id=1, source_target_pairs={{112,51},{0,67},{115,48},{3,64},{116,55},{4,71},{119,52},{7,68},{1... | collective-permute-start | bytes 1413128 | tf_op jit(solution)/shard_map/ppermute | solution.py:428
  82.0 20.8 %collective-permute-start.5 = (f32[10,23,1024]{2,1,0:T(8,128)S(1)}, f32[10,23,1024]{2,1,0:T(8,128)S(1)}, u32[]{:S(2)}, u32[]{:S(2)}) collective-permute-start(f32[10,23,1024]{2,1,0:T(8,128)S(1)} %get-tuple-element.19), channel_id=1, source_target_pairs={{0,16},{16,32},{32,48},{48,64},{64,80},{80,96},{96,112},{128,144},... | collective-permute-start | bytes 2826248 | tf_op jit(solution)/shard_map/ppermute | solution.py:432
  83.8 19.0 %collective-permute-start.6 = (f32[10,23,1024]{2,1,0:T(8,128)S(1)}, f32[10,23,1024]{2,1,0:T(8,128)S(1)}, u32[]{:S(2)}, u32[]{:S(2)}) collective-permute-start(f32[10,23,1024]{2,1,0:T(8,128)S(1)} %get-tuple-element.20), channel_id=1, source_target_pairs={{16,0},{32,16},{48,32},{64,48},{80,64},{96,80},{112,96},{144,128},... | collective-permute-start | bytes 2826248 | tf_op jit(solution)/shard_map/ppermute | solution.py:433
  85.1 0.7 collective-permute-start.9
  85.8 21.9 %collective-permute-start.11 = (f32[10,23,512]{2,1,0:T(8,128)S(1)}, f32[10,23,512]{2,1,0:T(8,128)S(1)}, u32[]{:S(2)}, u32[]{:S(2)}) collective-permute-start(f32[10,23,512]{2,1,0:T(8,128)S(1)} %collective-permute-done.10), channel_id=1, source_target_pairs={{18,129},{98,241},{17,130},{97,242},{22,133},{102,245},{21,134},{1... | collective-permute-start | bytes 1413128 | tf_op jit(solution)/shard_map/ppermute | solution.py:429
  87.1 20.5 %collective-permute-start.13 = (f32[10,23,512]{2,1,0:T(8,128)S(1)}, f32[10,23,512]{2,1,0:T(8,128)S(1)}, u32[]{:S(2)}, u32[]{:S(2)}) collective-permute-start(f32[10,23,512]{2,1,0:T(8,128)S(1)} %collective-permute-done.12), channel_id=1, source_target_pairs={{51,128},{67,240},{48,131},{64,243},{55,132},{71,244},{52,135},{68... | collective-permute-start | bytes 1413128 | tf_op jit(solution)/shard_map/ppermute | solution.py:429
  88.0 16.5 %collective-permute-start.3 = (bf16[66,16,128]{2,1,0:T(8,128)(2,1)S(1)}, bf16[66,16,128]{2,1,0:T(8,128)(2,1)S(1)}, u32[]{:S(2)}, u32[]{:S(2)}) collective-permute-start(bf16[66,16,128]{2,1,0:T(8,128)(2,1)S(1)} %shard_map.20), channel_id=1, source_target_pairs={{1,2},{2,1},{5,6},{6,5},{9,10},{10,9},{13,14},{14,13},{17,18},{18,... | collective-permute-start | bytes 811016 | tf_op jit(solution)/shard_map/ppermute | solution.py:389

commit v5 on v4

--- a/solution.py
+++ b/solution.py
@@ -108,13 +108,20 @@
         run(0, days - DAY_HALF)
 
 
-def pack_edge_kernel(own, off, on):
-    lons, days, width = own.shape
+def pack_edge_kernel(field, off, on, own, sems):
+    lons, days, width = field.shape
+    moves = []
+    for k, at in enumerate((0, lons - LON_HALF)):
+        part = own.at[k * LON_HALF : (k + 1) * LON_HALF]
+        moves.append(pltpu.make_async_copy(field.at[at : at + LON_HALF], part, sems.at[k]))
+        moves[-1].start()
+    for move in moves:
+        move.wait()
     cols = slice(0, width)
 
     def run(off_low, on_low):
-        pack_dense(own, 0, lons, off_low, cols, off)
-        pack_plain(own, 0, lons, on_low, cols, on)
+        pack_dense(own, 0, 2 * LON_HALF, off_low, cols, off)
+        pack_plain(own, 0, 2 * LON_HALF, on_low, cols, on)
 
     by_core(lax.axis_index("day") % 2, days, run)
 
@@ -341,7 +348,7 @@
                     buf[side, j, :, slice(at - base, at - base + block)] = value * SCALE
                     return 0
 
-                lax.fori_loop(0, LON_HALF, add, 0, unroll=5)
+                lax.fori_loop(0, LON_HALF, add, 0, unroll=True)
         moves.append(pltpu.make_async_copy(buf.at[side], out.at[row : row + LON_HALF, :, base : base + width], sems.at[side]))
         moves[-1].start()
     return moves
@@ -377,9 +384,16 @@
             compiler_params=params,
         )(*args)
 
-    ends_own = jnp.concatenate([field[:LON_HALF], field[lons - LON_HALF :]], axis=0)
-    shapes = [bf16(dense_tiles(2 * LON_HALF), DAY_PAD, cols), bf16(2 * LON_HALF, DAY_PAD, cols)]
-    e_off, e_on = call(pack_edge_kernel, [ends_own], shapes)
+    e_off, e_on = pl.pallas_call(
+        pack_edge_kernel,
+        in_specs=[ANY],
+        out_specs=[VMEM] * 2,
+        out_shape=[bf16(dense_tiles(2 * LON_HALF), DAY_PAD, cols), bf16(2 * LON_HALF, DAY_PAD, cols)],
+        scratch_shapes=[pltpu.VMEM((2 * LON_HALF, days, cols), field.dtype), pltpu.SemaphoreType.DMA((2,))],
+        cost_estimate=cost(1000),
+        compiler_params=pltpu.CompilerParams(vmem_limit_bytes=52 * 2**20),
+        name="packe",
+    )(field)
     edge_off = lax.ppermute(e_off, "day", swap(1, 2))
     edge_on = lax.ppermute(e_on, "day", swap(0, 2))
 
@@ -454,7 +468,7 @@
         scratch = [
             pltpu.VMEM((lons, days, block), jnp.float32),
             pltpu.VMEM((slots, lons if own_join else mid, days, block), jnp.float32),
-            pltpu.SemaphoreType.DMA((slots, 3 if own_join else 2)),
+            pltpu.SemaphoreType.DMA((slots, 5 if own_join else 2)),
         ]
         if joined:
             scratch += [pltpu.VMEM((2, LON_HALF, days, sum(WIDTHS[k] for k in joined)), jnp.float32), pltpu.SemaphoreType.DMA((2,))]

time: 110 us -> 110 us (level)
  Pallas kernels: 15.6 us -> 17.2 us
  local copies, waits for them, and re-layouts: 1.4 us -> 0.01 us
    pallas_call x0 -> x1, Pallas kernels: none -> 1.49 us  [local(): pl.pallas_call(pack_edge_kernel, in_specs=[ANY], out_specs=[VMEM] * 2, ou...]
    slice x1 -> x0, local copies, waits for them, and re-layouts: 1.39 us -> none  [local(): field[:LON_HALF]]
    pallas_call x8 -> x7, Pallas kernels: 7.25 us -> 7.09 us  [call(): pl.pallas_call(body, in_specs=[VMEM] * len(args), out_specs=[VMEM] * len(...]
  transfers between devices with their start and end apart: 17 -> 17, of which waited for: 6 -> 6; matrix products, arithmetic and copies ran while one was open for 0% -> 0% of each run, Pallas kernels for 12% -> 13%
where the time goes in v5:
time: 110 us; the launch traced here: 109 us
  waiting for transfers between devices  52 us (47%)
  starting transfers between devices  39.8 us (36%)
  Pallas kernels  17.2 us (16%)
    ppermute x1, waiting for transfers between devices, local(): edge_off = lax.ppermute(e_off, 'day', swap(1, 2))  28.5 us
    ppermute x4, waiting for transfers between devices, local(): mid_direct.append(lax.ppermute(off, 'day', swap(1, 4)))  12.9 us
    ppermute x4, starting transfers between devices, local(): mid_direct.append(lax.ppermute(off, 'day', swap(1, 4)))  12 us
    ppermute x1, starting transfers between devices, local(): landed.insert(0, lax.ppermute(first, both_axes, straight))  10.3 us
    pallas_call x4, Pallas kernels, local(): pl.pallas_call(fn, in_specs=specs, out_specs=[ANY] if own_join else [ANY,...  7.66 us
    ppermute x1, waiting for transfers between devices, local(): landed.insert(0, lax.ppermute(first, both_axes, straight))  7.14 us
    pallas_call x7, Pallas kernels, call(): pl.pallas_call(body, in_specs=[VMEM] * len(args), out_specs=[VMEM] * len(...  7.09 us
    ppermute x1, starting transfers between devices, local(): edge_on = lax.ppermute(e_on, 'day', swap(0, 2))  5.86 us
  transfers between devices with their start and end apart: 17, of which 6 were waited for; matrix products, arithmetic and copies ran while one was open for 0% of the time, Pallas kernels for 13%

profile of v5, /device:TPU:1, one launch (start us, length us, event | category | flops | bytes accessed | tf_op | source)
XLA Modules:
  0.0 109.3 jit_solution(1940200887706925237)
XLA Ops:
  0.0 1.5 %packe.1 = (bf16[19,16,1024]{2,1,0:T(8,128)(2,1)S(1)}, bf16[20,16,1024]{2,1,0:T(8,128)(2,1)S(1)}) custom-call(bf16[90,23,1024]{2,1,0:T(8,128)(2,1)} %bitcast.2), custom_call_target="tpu_custom_call" | custom-call | flops 1000000 | bytes 10000 | tf_op jit(solution)/shard_map/packe/pallas_call | solution.py:387
  1.5 2.8 %collective-permute-start = (bf16[19,16,1024]{2,1,0:T(8,128)(2,1)S(1)}, bf16[19,16,1024]{2,1,0:T(8,128)(2,1)S(1)}, u32[]{:S(2)}, u32[]{:S(2)}) collective-permute-start(bf16[19,16,1024]{2,1,0:T(8,128)(2,1)S(1)} %get-tuple-element.17), channel_id=1, source_target_pairs={{1,2},{2,1},{3,4},{4,3},{5,6},{6,5},{7,8},{8,7},{9,10},{10,9},{11,... | collective-permute-start | bytes 1867784 | tf_op jit(solution)/shard_map/ppermute | solution.py:397
  4.3 0.8 collective-permute-start.4
  5.1 5.9 %collective-permute-start.1 = (bf16[20,16,1024]{2,1,0:T(8,128)(2,1)S(1)}, bf16[20,16,1024]{2,1,0:T(8,128)(2,1)S(1)}, u32[]{:S(2)}, u32[]{:S(2)}) collective-permute-start(bf16[20,16,1024]{2,1,0:T(8,128)(2,1)S(1)} %get-tuple-element.18), channel_id=1, source_target_pairs={{0,1},{1,0},{2,3},{3,2},{4,5},{5,4},{6,7},{7,6},{8,9},{9,8},{10,11... | collective-permute-start | bytes 1966088 | tf_op jit(solution)/shard_map/ppermute | solution.py:398
  10.9 0.3 shard_map.17
  11.3 0.1 shard_map.22
  11.4 1.9 %collective-permute-start.15 = (bf16[66,16,512]{2,1,0:T(8,128)(2,1)S(1)}, bf16[66,16,512]{2,1,0:T(8,128)(2,1)S(1)}, u32[]{:S(2)}, u32[]{:S(2)}) collective-permute-start(bf16[66,16,512]{2,1,0:T(8,128)(2,1)S(1)} %shard_map.22), channel_id=1, source_target_pairs={{1,2},{2,1},{5,6},{6,5},{9,10},{10,9},{13,14},{14,13},{17,18},{18,... | collective-permute-start | bytes 3244040 | tf_op jit(solution)/shard_map/ppermute | solution.py:403
  13.5 28.5 %collective-permute-done.edge_off.off = bf16[19,16,1024]{2,1,0:T(8,128)(2,1)S(1)} collective-permute-done((bf16[19,16,1024]{2,1,0:T(8,128)(2,1)S(1)}, bf16[19,16,1024]{2,1,0:T(8,128)(2,1)S(1)}, u32[]{:S(2)}, u32[]{:S(2)}) %collective-permute-start) | collective-permute-done | bytes 622624 | tf_op jit(solution)/shard_map/ppermute | solution.py:397
  42.0 3.6 %collective-permute-start.16 = (bf16[66,16,128]{2,1,0:T(8,128)(2,1)S(1)}, bf16[66,16,128]{2,1,0:T(8,128)(2,1)S(1)}, u32[]{:S(2)}, u32[]{:S(2)}) collective-permute-start(bf16[66,16,128]{2,1,0:T(8,128)(2,1)S(1)} %shard_map.25), channel_id=1, source_target_pairs={{1,2},{2,1},{5,6},{6,5},{9,10},{10,9},{13,14},{14,13},{17,18},{18,... | collective-permute-start | bytes 811016 | tf_op jit(solution)/shard_map/ppermute | solution.py:403
  45.7 0.1 shard_map.21
  45.8 1.9 %collective-permute-start.14 = (bf16[66,16,256]{2,1,0:T(8,128)(2,1)S(1)}, bf16[66,16,256]{2,1,0:T(8,128)(2,1)S(1)}, u32[]{:S(2)}, u32[]{:S(2)}) collective-permute-start(bf16[66,16,256]{2,1,0:T(8,128)(2,1)S(1)} %shard_map.21), channel_id=1, source_target_pairs={{1,2},{2,1},{5,6},{6,5},{9,10},{10,9},{13,14},{14,13},{17,18},{18,... | collective-permute-start | bytes 1622024 | tf_op jit(solution)/shard_map/ppermute | solution.py:403
  47.7 1.0 edge.1
  48.7 8.1 %collective-permute-done.16.mid_direct = bf16[66,16,128]{2,1,0:T(8,128)(2,1)S(1)} collective-permute-done((bf16[66,16,128]{2,1,0:T(8,128)(2,1)S(1)}, bf16[66,16,128]{2,1,0:T(8,128)(2,1)S(1)}, u32[]{:S(2)}, u32[]{:S(2)}) %collective-permute-start.16) | collective-permute-done | bytes 270368 | tf_op jit(solution)/shard_map/ppermute | solution.py:403
  56.8 0.7 collective-permute-start.8
  57.5 4.8 %collective-permute-done.14.mid_direct = bf16[66,16,256]{2,1,0:T(8,128)(2,1)S(1)} collective-permute-done((bf16[66,16,256]{2,1,0:T(8,128)(2,1)S(1)}, bf16[66,16,256]{2,1,0:T(8,128)(2,1)S(1)}, u32[]{:S(2)}, u32[]{:S(2)}) %collective-permute-start.14) | collective-permute-done | bytes 540704 | tf_op jit(solution)/shard_map/ppermute | solution.py:403
  62.3 10.3 %collective-permute-start.7 = (f32[10,23,512]{2,1,0:T(8,128)S(1)}, f32[10,23,512]{2,1,0:T(8,128)S(1)}, u32[]{:S(2)}, u32[]{:S(2)}) collective-permute-start(f32[10,23,512]{2,1,0:T(8,128)S(1)} %get-tuple-element.21), channel_id=1, source_target_pairs={{113,129},{1,241},{114,130},{2,242},{117,133},{5,245},{118,134},{6... | collective-permute-start | bytes 1413128 | tf_op jit(solution)/shard_map/ppermute | solution.py:444
  72.6 1.3 %collective-permute-start.10 = (f32[10,23,512]{2,1,0:T(8,128)S(1)}, f32[10,23,512]{2,1,0:T(8,128)S(1)}, u32[]{:S(2)}, u32[]{:S(2)}) collective-permute-start(f32[10,23,512]{2,1,0:T(8,128)S(1)} %get-tuple-element.22), channel_id=1, source_target_pairs={{113,18},{1,98},{114,17},{2,97},{117,22},{5,102},{118,21},{6,101},... | collective-permute-start | bytes 1413128 | tf_op jit(solution)/shard_map/ppermute | solution.py:442
  73.9 0.7 collective-permute-start.12
  74.6 7.1 %collective-permute-done.7.rest_2_ = f32[10,23,512]{2,1,0:T(8,128)S(1)} collective-permute-done((f32[10,23,512]{2,1,0:T(8,128)S(1)}, f32[10,23,512]{2,1,0:T(8,128)S(1)}, u32[]{:S(2)}, u32[]{:S(2)}) %collective-permute-start.7) | collective-permute-done | bytes 471072 | tf_op jit(solution)/shard_map/ppermute | solution.py:444
  81.8 1.3 %collective-permute-start.5 = (f32[10,23,1024]{2,1,0:T(8,128)S(1)}, f32[10,23,1024]{2,1,0:T(8,128)S(1)}, u32[]{:S(2)}, u32[]{:S(2)}) collective-permute-start(f32[10,23,1024]{2,1,0:T(8,128)S(1)} %get-tuple-element.19), channel_id=1, source_target_pairs={{0,16},{16,32},{32,48},{48,64},{64,80},{80,96},{96,112},{128,144},... | collective-permute-start | bytes 2826248 | tf_op jit(solution)/shard_map/ppermute | solution.py:446
  83.1 0.5 collective-permute-done.10
  83.6 1.3 %collective-permute-start.6 = (f32[10,23,1024]{2,1,0:T(8,128)S(1)}, f32[10,23,1024]{2,1,0:T(8,128)S(1)}, u32[]{:S(2)}, u32[]{:S(2)}) collective-permute-start(f32[10,23,1024]{2,1,0:T(8,128)S(1)} %get-tuple-element.20), channel_id=1, source_target_pairs={{16,0},{32,16},{48,32},{64,48},{80,64},{96,80},{112,96},{144,128},... | collective-permute-start | bytes 2826248 | tf_op jit(solution)/shard_map/ppermute | solution.py:447
  84.9 0.7 collective-permute-start.9
  85.6 1.3 %collective-permute-start.11 = (f32[10,23,512]{2,1,0:T(8,128)S(1)}, f32[10,23,512]{2,1,0:T(8,128)S(1)}, u32[]{:S(2)}, u32[]{:S(2)}) collective-permute-start(f32[10,23,512]{2,1,0:T(8,128)S(1)} %collective-permute-done.10), channel_id=1, source_target_pairs={{18,129},{98,241},{17,130},{97,242},{22,133},{102,245},{21,134},{1... | collective-permute-start | bytes 1413128 | tf_op jit(solution)/shard_map/ppermute | solution.py:443
  86.9 0.7 collective-permute-start.13
  87.8 4.5 %collective-permute-start.3 = (bf16[66,16,128]{2,1,0:T(8,128)(2,1)S(1)}, bf16[66,16,128]{2,1,0:T(8,128)(2,1)S(1)}, u32[]{:S(2)}, u32[]{:S(2)}) collective-permute-start(bf16[66,16,128]{2,1,0:T(8,128)(2,1)S(1)} %shard_map.19), channel_id=1, source_target_pairs={{1,2},{2,1},{5,6},{6,5},{9,10},{10,9},{13,14},{14,13},{17,18},{18,... | collective-permute-start | bytes 811016 | tf_op jit(solution)/shard_map/ppermute | solution.py:403
  92.3 6.3 %shard_map.18.refs_0_.pre = f32[90,23,1024]{2,1,0:T(8,128)S(1)} custom-call(bf16[90,23,1024]{2,1,0:T(8,128)(2,1)S(1)} %bitcast.10, bf16[19,16,1024]{2,1,0:T(8,128)(2,1)S(1)} %collective-permute-done.edge_off.off, bf16[20,16,1024]{2,1,0:T(8,128)(2,1)S(1)} %collective-permute-done.1.edge_on.on, bf16[70,16,1024]{2,1,0:T(8,128)(2,1)S(1)} %collective-permute-done.2.mid_on), custom_call_target="tpu_custom_call" | custom-call | flops 9000000 | bytes 90000 | tf_op jit(solution)/shard_map/pallas_call | solution.py:378
  98.6 2.4 %shard_map.23 = (f32[90,23,1024]{2,1,0:T(8,128)}, f32[20,23,512]{2,1,0:T(8,128)S(1)}) custom-call(f32[90,23,1024]{2,1,0:T(8,128)S(1)} %shard_map.18.refs_0_.pre, bf16[66,16,512]{2,1,0:T(8,128)(2,1)S(1)} %collective-permute-done.15.refs_1_, bf16[66,16,1024]{2,1,0:T(8,128)(2,1)S(1)} %collective-permute-done.4.refs_2_.mid_diag), custom_call_target="tpu_custom_call" | custom-call | flops 5000000 | bytes 50000 | tf_op jit(solution)/shard_map/pallas_call | solution.py:476
  101.0 1.7 %shard_map.24 = (f32[90,23,1024]{2,1,0:T(8,128)}, f32[20,23,256]{2,1,0:T(8,128)S(1)}) custom-call(f32[90,23,1024]{2,1,0:T(8,128)S(1)} %shard_map.18.refs_0_.pre, bf16[66,16,256]{2,1,0:T(8,128)(2,1)S(1)} %collective-permute-done.14.mid_direct, bf16[66,16,1024]{2,1,0:T(8,128)(2,1)S(1)} %collective-permute-done.4.refs_2_.mid_diag, ...), custom_call_target="tpu_custom_call", output_to_operand_aliasing={{0}: (3, {})} | custom-call | flops 5000000 | bytes 50000 | tf_op jit(solution)/shard_map/pallas_call | solution.py:476
  102.7 1.8 %shard_map.26 = (f32[90,23,1024]{2,1,0:T(8,128)}, f32[20,23,128]{2,1,0:T(8,128)S(1)}) custom-call(f32[90,23,1024]{2,1,0:T(8,128)S(1)} %shard_map.18.refs_0_.pre, bf16[66,16,128]{2,1,0:T(8,128)(2,1)S(1)} %collective-permute-done.16.mid_direct, bf16[66,16,1024]{2,1,0:T(8,128)(2,1)S(1)} %collective-permute-done.4.refs_2_.mid_diag, ...), custom_call_target="tpu_custom_call", output_to_operand_aliasing={{0}: (8, {})} | custom-call | flops 5000000 | bytes 50000 | tf_op jit(solution)/shard_map/pallas_call | solution.py:476
  104.5 2.9 %collective-permute-done.11.rest_4_ = f32[10,23,512]{2,1,0:T(8,128)S(1)} collective-permute-done((f32[10,23,512]{2,1,0:T(8,128)S(1)}, f32[10,23,512]{2,1,0:T(8,128)S(1)}, u32[]{:S(2)}, u32[]{:S(2)}) %collective-permute-start.11) | collective-permute-done | bytes 471072 | tf_op jit(solution)/shard_map/ppermute | solution.py:443
  107.5 1.8 %shard_map.27 = f32[90,23,1024]{2,1,0:T(8,128)} custom-call(f32[90,23,1024]{2,1,0:T(8,128)S(1)} %shard_map.18.refs_0_.pre, bf16[66,16,128]{2,1,0:T(8,128)(2,1)S(1)} %collective-permute-done.3.mid_direct, bf16[66,16,1024]{2,1,0:T(8,128)(2,1)S(1)} %collective-permute-done.4.refs_2_.mid_diag, ...), custom_call_target="tpu_custom_call", output_to_operand_aliasing={{}: (11, {})} | custom-call | flops 5000000 | bytes 50000 | tf_op jit(solution)/shard_map/pallas_call | solution.py:476
  (17 shorter events, 0.4 us)
Async XLA Ops:
  0.0 4.3 %copy-start = (bf16[23,90,1024]{2,0,1:T(8,128)(2,1)S(1)}, bf16[23,90,1024]{2,0,1:T(8,128)(2,1)}, u32[]{:S(2)}) copy-start(bf16[23,90,1024]{2,0,1:T(8,128)(2,1)} %param.1) | copy-start | bytes 12718084
  1.5 40.5 %collective-permute-start = (bf16[19,16,1024]{2,1,0:T(8,128)(2,1)S(1)}, bf16[19,16,1024]{2,1,0:T(8,128)(2,1)S(1)}, u32[]{:S(2)}, u32[]{:S(2)}) collective-permute-start(bf16[19,16,1024]{2,1,0:T(8,128)(2,1)S(1)} %get-tuple-element.17), channel_id=1, source_target_pairs={{1,2},{2,1},{3,4},{4,3},{5,6},{6,5},{7,8},{8,7},{9,10},{10,9},{11,... | collective-permute-start | bytes 1867784 | tf_op jit(solution)/shard_map/ppermute | solution.py:397
  4.3 82.7 %collective-permute-start.4 = (bf16[66,16,1024]{2,1,0:T(8,128)(2,1)S(1)}, bf16[66,16,1024]{2,1,0:T(8,128)(2,1)S(1)}, u32[]{:S(2)}, u32[]{:S(2)}) collective-permute-start(bf16[66,16,1024]{2,1,0:T(8,128)(2,1)S(1)} %shard_map.20), channel_id=1, source_target_pairs={{3,4},{4,3},{7,8},{8,7},{11,12},{12,11},{15,0},{0,15},{19,20},{20,... | collective-permute-start | bytes 6488072 | tf_op jit(solution)/shard_map/ppermute | solution.py:418
  5.1 40.7 %collective-permute-start.1 = (bf16[20,16,1024]{2,1,0:T(8,128)(2,1)S(1)}, bf16[20,16,1024]{2,1,0:T(8,128)(2,1)S(1)}, u32[]{:S(2)}, u32[]{:S(2)}) collective-permute-start(bf16[20,16,1024]{2,1,0:T(8,128)(2,1)S(1)} %get-tuple-element.18), channel_id=1, source_target_pairs={{0,1},{1,0},{2,3},{3,2},{4,5},{5,4},{6,7},{7,6},{8,9},{9,8},{10,11... | collective-permute-start | bytes 1966088 | tf_op jit(solution)/shard_map/ppermute | solution.py:398
  11.2 76.6 %collective-permute-start.2 = (bf16[70,16,1024]{2,1,0:T(8,128)(2,1)S(1)}, bf16[70,16,1024]{2,1,0:T(8,128)(2,1)S(1)}, u32[]{:S(2)}, u32[]{:S(2)}) collective-permute-start(bf16[70,16,1024]{2,1,0:T(8,128)(2,1)S(1)} %shard_map.17), channel_id=1, source_target_pairs={{0,1},{1,0},{2,3},{3,2},{4,5},{5,4},{6,7},{7,6},{8,9},{9,8},{10,11... | collective-permute-start | bytes 6881288 | tf_op jit(solution)/shard_map/ppermute | solution.py:417
  11.4 61.1 %collective-permute-start.15 = (bf16[66,16,512]{2,1,0:T(8,128)(2,1)S(1)}, bf16[66,16,512]{2,1,0:T(8,128)(2,1)S(1)}, u32[]{:S(2)}, u32[]{:S(2)}) collective-permute-start(bf16[66,16,512]{2,1,0:T(8,128)(2,1)S(1)} %shard_map.22), channel_id=1, source_target_pairs={{1,2},{2,1},{5,6},{6,5},{9,10},{10,9},{13,14},{14,13},{17,18},{18,... | collective-permute-start | bytes 3244040 | tf_op jit(solution)/shard_map/ppermute | solution.py:403
  42.0 14.8 %collective-permute-start.16 = (bf16[66,16,128]{2,1,0:T(8,128)(2,1)S(1)}, bf16[66,16,128]{2,1,0:T(8,128)(2,1)S(1)}, u32[]{:S(2)}, u32[]{:S(2)}) collective-permute-start(bf16[66,16,128]{2,1,0:T(8,128)(2,1)S(1)} %shard_map.25), channel_id=1, source_target_pairs={{1,2},{2,1},{5,6},{6,5},{9,10},{10,9},{13,14},{14,13},{17,18},{18,... | collective-permute-start | bytes 811016 | tf_op jit(solution)/shard_map/ppermute | solution.py:403
  45.8 16.5 %collective-permute-start.14 = (bf16[66,16,256]{2,1,0:T(8,128)(2,1)S(1)}, bf16[66,16,256]{2,1,0:T(8,128)(2,1)S(1)}, u32[]{:S(2)}, u32[]{:S(2)}) collective-permute-start(bf16[66,16,256]{2,1,0:T(8,128)(2,1)S(1)} %shard_map.21), channel_id=1, source_target_pairs={{1,2},{2,1},{5,6},{6,5},{9,10},{10,9},{13,14},{14,13},{17,18},{18,... | collective-permute-start | bytes 1622024 | tf_op jit(solution)/shard_map/ppermute | solution.py:403
  56.8 17.1 %collective-permute-start.8 = (f32[10,23,512]{2,1,0:T(8,128)S(1)}, f32[10,23,512]{2,1,0:T(8,128)S(1)}, u32[]{:S(2)}, u32[]{:S(2)}) collective-permute-start(f32[10,23,512]{2,1,0:T(8,128)S(1)} %get-tuple-element.21), channel_id=1, source_target_pairs={{112,35},{0,83},{115,32},{3,80},{116,39},{4,87},{119,36},{7,84},{1... | collective-permute-start | bytes 1413128 | tf_op jit(solution)/shard_map/ppermute | solution.py:442
  62.3 19.5 %collective-permute-start.7 = (f32[10,23,512]{2,1,0:T(8,128)S(1)}, f32[10,23,512]{2,1,0:T(8,128)S(1)}, u32[]{:S(2)}, u32[]{:S(2)}) collective-permute-start(f32[10,23,512]{2,1,0:T(8,128)S(1)} %get-tuple-element.21), channel_id=1, source_target_pairs={{113,129},{1,241},{114,130},{2,242},{117,133},{5,245},{118,134},{6... | collective-permute-start | bytes 1413128 | tf_op jit(solution)/shard_map/ppermute | solution.py:444
  72.6 11.0 %collective-permute-start.10 = (f32[10,23,512]{2,1,0:T(8,128)S(1)}, f32[10,23,512]{2,1,0:T(8,128)S(1)}, u32[]{:S(2)}, u32[]{:S(2)}) collective-permute-start(f32[10,23,512]{2,1,0:T(8,128)S(1)} %get-tuple-element.22), channel_id=1, source_target_pairs={{113,18},{1,98},{114,17},{2,97},{117,22},{5,102},{118,21},{6,101},... | collective-permute-start | bytes 1413128 | tf_op jit(solution)/shard_map/ppermute | solution.py:442
  73.9 11.0 %collective-permute-start.12 = (f32[10,23,512]{2,1,0:T(8,128)S(1)}, f32[10,23,512]{2,1,0:T(8,128)S(1)}, u32[]{:S(2)}, u32[]{:S(2)}) collective-permute-start(f32[10,23,512]{2,1,0:T(8,128)S(1)} %get-tuple-element.22), channel_id=1, source_target_pairs={{112,51},{0,67},{115,48},{3,64},{116,55},{4,71},{119,52},{7,68},{1... | collective-permute-start | bytes 1413128 | tf_op jit(solution)/shard_map/ppermute | solution.py:442
  81.8 20.9 %collective-permute-start.5 = (f32[10,23,1024]{2,1,0:T(8,128)S(1)}, f32[10,23,1024]{2,1,0:T(8,128)S(1)}, u32[]{:S(2)}, u32[]{:S(2)}) collective-permute-start(f32[10,23,1024]{2,1,0:T(8,128)S(1)} %get-tuple-element.19), channel_id=1, source_target_pairs={{0,16},{16,32},{32,48},{48,64},{64,80},{80,96},{96,112},{128,144},... | collective-permute-start | bytes 2826248 | tf_op jit(solution)/shard_map/ppermute | solution.py:446
  83.6 19.1 %collective-permute-start.6 = (f32[10,23,1024]{2,1,0:T(8,128)S(1)}, f32[10,23,1024]{2,1,0:T(8,128)S(1)}, u32[]{:S(2)}, u32[]{:S(2)}) collective-permute-start(f32[10,23,1024]{2,1,0:T(8,128)S(1)} %get-tuple-element.20), channel_id=1, source_target_pairs={{16,0},{32,16},{48,32},{64,48},{80,64},{96,80},{112,96},{144,128},... | collective-permute-start | bytes 2826248 | tf_op jit(solution)/shard_map/ppermute | solution.py:447
  84.9 0.7 collective-permute-start.9
  85.6 21.8 %collective-permute-start.11 = (f32[10,23,512]{2,1,0:T(8,128)S(1)}, f32[10,23,512]{2,1,0:T(8,128)S(1)}, u32[]{:S(2)}, u32[]{:S(2)}) collective-permute-start(f32[10,23,512]{2,1,0:T(8,128)S(1)} %collective-permute-done.10), channel_id=1, source_target_pairs={{18,129},{98,241},{17,130},{97,242},{22,133},{102,245},{21,134},{1... | collective-permute-start | bytes 1413128 | tf_op jit(solution)/shard_map/ppermute | solution.py:443
  86.9 20.5 %collective-permute-start.13 = (f32[10,23,512]{2,1,0:T(8,128)S(1)}, f32[10,23,512]{2,1,0:T(8,128)S(1)}, u32[]{:S(2)}, u32[]{:S(2)}) collective-permute-start(f32[10,23,512]{2,1,0:T(8,128)S(1)} %collective-permute-done.12), channel_id=1, source_target_pairs={{51,128},{67,240},{48,131},{64,243},{55,132},{71,244},{52,135},{68... | collective-permute-start | bytes 1413128 | tf_op jit(solution)/shard_map/ppermute | solution.py:443
  87.8 16.7 %collective-permute-start.3 = (bf16[66,16,128]{2,1,0:T(8,128)(2,1)S(1)}, bf16[66,16,128]{2,1,0:T(8,128)(2,1)S(1)}, u32[]{:S(2)}, u32[]{:S(2)}) collective-permute-start(bf16[66,16,128]{2,1,0:T(8,128)(2,1)S(1)} %shard_map.19), channel_id=1, source_target_pairs={{1,2},{2,1},{5,6},{6,5},{9,10},{10,9},{13,14},{14,13},{17,18},{18,... | collective-permute-start | bytes 811016 | tf_op jit(solution)/shard_map/ppermute | solution.py:403
